TPU v7x, 256 devices: a whole 4x4x8 slice. The times are simulated.
256 devices in a mesh: gz: 2 (over core), gx: 8 (over y, x_hi), gy: 16 (over z, x_lo).
Axes of the slice: x: 4 (x_hi: 2, x_lo: 2; x = x_hi * 2 + x_lo), y: 4, z: 8, core: 2. Of those that a mesh axis runs over, the one named last changes fastest.
Arguments:
- queries: bfloat16 [2, 16384, 128], P('gz', 'gx'), may hold values from -6 to 6
- keys: bfloat16 [2, 16384, 128], P('gz', 'gy'), may hold values from -6 to 6
- values: bfloat16 [2, 16384, 128], P('gz', 'gy'), may hold values from -6 to 6
- w_out: bfloat16 [256, 2048], replicated, may hold values from -0.375 to 0.375
Outputs:
- mixed: bfloat16 [16384, 2048], P(('gx', 'gy'), 'gz')
All inputs are finite; a program needn't handle non-finite values.
Results may differ from a plain program's by a relative error of at most 0.02.
Values may be sent and summed in bfloat16 or wider, within the bound.
A program may use at most 64 MiB of HBM per device.

v0:
```python
import math

import jax
import jax.numpy as jnp
from jax import lax
from jax.sharding import PartitionSpec as P

SWEEPS = 3


def copy_for_each(x, axis):
    copies = jnp.broadcast_to(x, (lax.axis_size(axis), *x.shape))
    return lax.all_to_all(copies, axis, split_axis=0, concat_axis=0, tiled=True)


def all_in_one(x, axis):
    leaves = jax.tree.leaves(x)
    turns = sorted(range(len(leaves)), key=lambda k: -leaves[k].size)
    width = (1, *leaves[turns[0]].shape)[-1]
    lines = [
        jnp.pad(leaves[k].reshape(-1), (0, -leaves[k].size % width)).reshape(-1, width)
        for k in turns
    ]
    both, at, found = (copy_for_each(jnp.concatenate(lines), axis), 0, {})
    for k, line in zip(turns, lines):
        share = both[:, at : at + len(line)].reshape(len(both), -1)
        found[k] = share[:, : leaves[k].size].reshape(-1, *leaves[k].shape)
        at += len(line)
    numbers = iter(range(len(leaves)))
    return jax.tree.map(lambda _: found[next(numbers)], x)


def collected_alike(x, axis):
    leaves, found = (jax.tree.leaves(x), {})
    for leading, a in enumerate(leaves):
        if leading not in found:
            alike = [k for k, b in enumerate(leaves) if b.dtype == a.dtype]
            got = (
                all_in_one([leaves[k] for k in alike], axis)
                if len(alike) > 1
                else [copy_for_each(a, axis)]
            )
            for k, b in zip(alike, got):
                found[k] = b
    numbers = iter(range(len(leaves)))
    return jax.tree.map(lambda _: found[next(numbers)], x)


def joined_by_halves(pieces, combine):
    while len(jax.tree.leaves(pieces)[0]) > 1:
        pieces = jax.vmap(combine)(
            *(jax.tree.map(lambda part: part[side::2], pieces) for side in (0, 1))
        )
    return jax.tree.map(lambda part: part[0], pieces)


def combined_all(x, axis, combine):
    pieces = collected_alike(x, axis)
    return joined_by_halves(pieces, combine)


def joined_all(x, axis, combine):
    pieces = all_in_one(x, axis)
    return joined_by_halves(pieces, combine)


def split_up(x, dim, size):
    before, after = (x.shape[:dim], x.shape[dim + 1 :])
    return jnp.moveaxis(x.reshape(*before, size, -1, *after), dim, 0)


def sum_at_owner(x, axis, dim):
    size = lax.axis_size(axis)
    tiles = lax.all_to_all(split_up(x, dim, size), axis, 0, 0, tiled=True)
    return jnp.sum(tiles.astype(jnp.float32), axis=0)


def in_order(tiles, dim):
    tiles = jnp.moveaxis(tiles, 0, dim)
    lengths = tiles.shape
    return tiles.reshape(*lengths[:dim], lengths[dim] * lengths[dim + 1], *lengths[dim + 2 :])


def gathered_copies(x, axis, dim):
    tiles = copy_for_each(x, axis)
    return in_order(tiles, dim)


def combine(first, second):
    biggest = jnp.maximum(first[0], second[0])
    return (
        biggest,
        first[1] * jnp.exp(first[0] - biggest) + second[1] * jnp.exp(second[0] - biggest),
    )


def row_log_total(local_max, local_sum):
    biggest, summed = combined_all((local_max, local_sum), "gy", combine)
    return biggest + jnp.log(summed)


def col_log_total(local_max, local_sum):
    biggest, summed = joined_all((local_max, local_sum), "gx", combine)
    return biggest + jnp.log(summed)


def body(queries, keys, values, w_out):
    head_count, row_count, head_width = queries.shape
    key_count = keys.shape[1]
    score_scale = 1.0 / math.sqrt(head_width)
    block_rows = min(512, row_count)
    block_total = row_count // block_rows
    block_ids = jnp.arange(block_total)

    def scores_at(block_index):
        query_block = lax.dynamic_slice_in_dim(queries, block_index * block_rows, block_rows, 1)
        return (
            jnp.einsum("hqd,hkd->hqk", query_block, keys, preferred_element_type=jnp.float32)
            * score_scale
        )

    def row_step(col_pot):

        def row_one_block(block_index):
            shifted = scores_at(block_index) + col_pot[:, None, :]
            biggest = jnp.max(shifted, axis=2)
            summed = jnp.sum(jnp.exp(shifted - biggest[:, :, None]), axis=2)
            return (biggest, summed)

        biggest, summed = lax.map(row_one_block, block_ids)
        biggest = jnp.transpose(biggest, (1, 0, 2)).reshape(head_count, row_count)
        summed = jnp.transpose(summed, (1, 0, 2)).reshape(head_count, row_count)
        return -row_log_total(biggest, summed)

    def col_step(row_pot):

        def col_one_block(block_index, state):
            biggest, summed = state
            row_block = lax.dynamic_slice_in_dim(row_pot, block_index * block_rows, block_rows, 1)
            shifted = scores_at(block_index) + row_block[:, :, None]
            larger = jnp.maximum(biggest, jnp.max(shifted, axis=1))
            summed = summed * jnp.exp(biggest - larger) + jnp.sum(
                jnp.exp(shifted - larger[:, None, :]), axis=1
            )
            return (larger, summed)

        start_state = (
            jnp.full((head_count, key_count), -1e30, jnp.float32),
            jnp.zeros((head_count, key_count), jnp.float32),
        )
        biggest, summed = lax.fori_loop(0, block_total, col_one_block, start_state)
        return -col_log_total(biggest, summed)

    col_pot = jnp.zeros((head_count, key_count), jnp.float32)
    for sweep_index in range(SWEEPS):
        row_pot = row_step(col_pot)
        col_pot = col_step(row_pot)
    row_pot = row_step(col_pot)

    def value_block(block_index):
        row_block = lax.dynamic_slice_in_dim(row_pot, block_index * block_rows, block_rows, 1)
        weights = jnp.exp(
            scores_at(block_index) + row_block[:, :, None] + col_pot[:, None, :]
        ).astype(jnp.bfloat16)
        return jnp.einsum("hqk,hkd->hqd", weights, values, preferred_element_type=jnp.float32)

    partial_value = lax.map(value_block, block_ids)
    partial_value = jnp.transpose(partial_value, (1, 0, 2, 3)).reshape(
        head_count, row_count, head_width
    )
    own_count = row_count // lax.axis_size("gy")
    own_rows = sum_at_owner(partial_value.astype(jnp.bfloat16), "gy", 1)
    head_out = own_rows.astype(jnp.bfloat16)
    flat_heads = jnp.transpose(head_out, (1, 0, 2)).reshape(own_count, head_count * head_width)
    model_width = w_out.shape[1]
    column_count = model_width // lax.axis_size("gz")
    position = lax.axis_index("gz")
    w_columns = lax.dynamic_slice_in_dim(w_out, position * column_count, column_count, 1)
    mixed = jnp.dot(
        gathered_copies(flat_heads, "gz", 1), w_columns, preferred_element_type=jnp.float32
    )
    return mixed.astype(jnp.bfloat16)


def solution(mesh):
    return jax.shard_map(
        body,
        mesh=mesh,
        in_specs=(P("gz", "gx", None), P("gz", "gy", None), P("gz", "gy", None), P()),
        out_specs=P(("gx", "gy"), "gz"),
        check_vma=False,
    )
```

profile of v0, /device:TPU:1, one launch (start us, length us, event | category | flops | bytes accessed | tf_op | source)
XLA Modules:
  0.0 224.7 jit_solution(3847837066673121247)
XLA Ops:
  0.0 13.8 %while.106 = (s32[]{:T(128)}, f32[4,1,512]{2,1,0:T(1,128)S(1)}, f32[4,1,512]{2,1,0:T(1,128)S(1)}, s32[4]{0:T(128)S(1)}, bf16[1,2048,128]{2,1,0:T(8,128)(2,1)}, /...) while((s32[]{:T(128)}, f32[4,1,512]{2,1,0:T(1,128)S(1)}, ...), condition=%wide.region_3.4_spmd, body=%wide.region_0.3_spmd.sunk | while | flops 136838144 | bytes 4602023 | solution.py:130
  1.4 1.5 multiply_reduce_fusion.2
  4.9 1.5 multiply_reduce_fusion.2
  8.3 1.5 multiply_reduce_fusion.2
  14.7 10.0 %all-to-all-start = ((f32[16,2,2048]{2,1,0:T(2,128)}), f32[16,2,2048]{2,1,0:T(2,128)S(1)}, u32[]{:S(2)}, u32[]{:S(2)}) async-start(f32[16,2,2048]{2,1,0:T(2,128)} %broadcast_in_dim.84), calls=%async_computation | async-start | bytes 524288 | tf_op jit(solution)/shard_map/all_to_all | solution.py:13
  24.8 10.6 %all-to-all-done = f32[16,2,2048]{2,1,0:T(2,128)S(1)} async-done(((f32[16,2,2048]{2,1,0:T(2,128)}), f32[16,2,2048]{2,1,0:T(2,128)S(1)}, u32[]{:S(2)}, u32[]{:S(2)}) %all-to-all-start) | async-done | bytes 262176 | tf_op jit(solution)/shard_map/all_to_all | solution.py:13
  36.0 7.8 %while.111 = (s32[]{:T(128)}, f32[1,1024]{1,0:T(1,128)S(1)}, f32[1,1024]{1,0:T(1,128)S(1)}, bf16[1,2048,128]{2,1,0:T(8,128)(2,1)}, bf16[1,1024,128]{2,1,0:T(8,12...) while((s32[]{:T(128)}, f32[1,1024]{1,0:T(1,128)S(1)}, ...), condition=%wide.region_7.8_spmd.clone, body=%wide.region_4.7_spmd.clone.sunk | while | flops 137892864 | bytes 4649126 | solution.py:151
  44.5 6.4 %all-to-all-start.1 = ((f32[8,2,1024]{2,1,0:T(2,128)}), f32[8,2,1024]{2,1,0:T(2,128)S(1)}, u32[]{:S(2)}, u32[]{:S(2)}) async-start(f32[8,2,1024]{2,1,0:T(2,128)} %broadcast_in_dim.85), calls=%async_computation.1 | async-start | bytes 131072 | tf_op jit(solution)/shard_map/all_to_all | solution.py:13
  50.8 6.7 %all-to-all-done.1 = f32[8,2,1024]{2,1,0:T(2,128)S(1)} async-done(((f32[8,2,1024]{2,1,0:T(2,128)}), f32[8,2,1024]{2,1,0:T(2,128)S(1)}, u32[]{:S(2)}, u32[]{:S(2)}) %all-to-all-start.1) | async-done | bytes 65568 | tf_op jit(solution)/shard_map/all_to_all | solution.py:13
  57.8 13.2 %while.107 = (s32[]{:T(128)}, f32[4,1,512]{2,1,0:T(1,128)S(1)}, f32[4,1,512]{2,1,0:T(1,128)S(1)}, s32[4]{0:T(128)S(1)}, bf16[1,2048,128]{2,1,0:T(8,128)(2,1)}, /...) while((s32[]{:T(128)}, f32[4,1,512]{2,1,0:T(1,128)S(1)}, ...), condition=%wide.region_11.12_spmd, body=%wide.region_8.11_spmd.sunk | while | flops 137886720 | bytes 4610223 | solution.py:130
  71.7 3.5 %all-to-all-start.2 = ((f32[16,2,2048]{2,1,0:T(2,128)}), f32[16,2,2048]{2,1,0:T(2,128)S(1)}, u32[]{:S(2)}, u32[]{:S(2)}) async-start(f32[16,2,2048]{2,1,0:T(2,128)} %broadcast_in_dim.86), calls=%async_computation.2 | async-start | bytes 524288 | tf_op jit(solution)/shard_map/all_to_all | solution.py:13
  75.3 9.9 %all-to-all-done.2 = f32[16,2,2048]{2,1,0:T(2,128)S(1)} async-done(((f32[16,2,2048]{2,1,0:T(2,128)}), f32[16,2,2048]{2,1,0:T(2,128)S(1)}, u32[]{:S(2)}, u32[]{:S(2)}) %all-to-all-start.2) | async-done | bytes 262176 | tf_op jit(solution)/shard_map/all_to_all | solution.py:13
  85.8 7.8 %while.112 = (s32[]{:T(128)}, f32[1,1024]{1,0:T(1,128)S(1)}, f32[1,1024]{1,0:T(1,128)S(1)}, bf16[1,2048,128]{2,1,0:T(8,128)(2,1)}, bf16[1,1024,128]{2,1,0:T(8,12...) while((s32[]{:T(128)}, f32[1,1024]{1,0:T(1,128)S(1)}, ...), condition=%wide.region_15.16_spmd.clone, body=%wide.region_12.15_spmd.clone.sunk | while | flops 137892864 | bytes 4649126 | solution.py:151
  94.3 3.4 %all-to-all-start.3 = ((f32[8,2,1024]{2,1,0:T(2,128)}), f32[8,2,1024]{2,1,0:T(2,128)S(1)}, u32[]{:S(2)}, u32[]{:S(2)}) async-start(f32[8,2,1024]{2,1,0:T(2,128)} %broadcast_in_dim.87), calls=%async_computation.3 | async-start | bytes 131072 | tf_op jit(solution)/shard_map/all_to_all | solution.py:13
  97.7 6.6 %all-to-all-done.3 = f32[8,2,1024]{2,1,0:T(2,128)S(1)} async-done(((f32[8,2,1024]{2,1,0:T(2,128)}), f32[8,2,1024]{2,1,0:T(2,128)S(1)}, u32[]{:S(2)}, u32[]{:S(2)}) %all-to-all-start.3) | async-done | bytes 65568 | tf_op jit(solution)/shard_map/all_to_all | solution.py:13
  104.5 13.2 %while.108 = (s32[]{:T(128)}, f32[4,1,512]{2,1,0:T(1,128)S(1)}, f32[4,1,512]{2,1,0:T(1,128)S(1)}, s32[4]{0:T(128)S(1)}, bf16[1,2048,128]{2,1,0:T(8,128)(2,1)}, /...) while((s32[]{:T(128)}, f32[4,1,512]{2,1,0:T(1,128)S(1)}, ...), condition=%wide.region_19.20_spmd, body=%wide.region_16.19_spmd.sunk | while | flops 137886720 | bytes 4610223 | solution.py:130
  118.5 3.5 %all-to-all-start.4 = ((f32[16,2,2048]{2,1,0:T(2,128)}), f32[16,2,2048]{2,1,0:T(2,128)S(1)}, u32[]{:S(2)}, u32[]{:S(2)}) async-start(f32[16,2,2048]{2,1,0:T(2,128)} %broadcast_in_dim.88), calls=%async_computation.4 | async-start | bytes 524288 | tf_op jit(solution)/shard_map/all_to_all | solution.py:13
  122.1 9.9 %all-to-all-done.4 = f32[16,2,2048]{2,1,0:T(2,128)S(1)} async-done(((f32[16,2,2048]{2,1,0:T(2,128)}), f32[16,2,2048]{2,1,0:T(2,128)S(1)}, u32[]{:S(2)}, u32[]{:S(2)}) %all-to-all-start.4) | async-done | bytes 262176 | tf_op jit(solution)/shard_map/all_to_all | solution.py:13
  132.6 7.8 %while.113 = (s32[]{:T(128)}, f32[1,1024]{1,0:T(1,128)S(1)}, f32[1,1024]{1,0:T(1,128)S(1)}, bf16[1,2048,128]{2,1,0:T(8,128)(2,1)}, bf16[1,1024,128]{2,1,0:T(8,12...) while((s32[]{:T(128)}, f32[1,1024]{1,0:T(1,128)S(1)}, ...), condition=%wide.region_23.24_spmd.clone, body=%wide.region_20.23_spmd.clone.sunk | while | flops 137892864 | bytes 4649126 | solution.py:151
  141.1 3.4 %all-to-all-start.5 = ((f32[8,2,1024]{2,1,0:T(2,128)}), f32[8,2,1024]{2,1,0:T(2,128)S(1)}, u32[]{:S(2)}, u32[]{:S(2)}) async-start(f32[8,2,1024]{2,1,0:T(2,128)} %broadcast_in_dim.89), calls=%async_computation.5 | async-start | bytes 131072 | tf_op jit(solution)/shard_map/all_to_all | solution.py:13
  144.4 6.6 %all-to-all-done.5 = f32[8,2,1024]{2,1,0:T(2,128)S(1)} async-done(((f32[8,2,1024]{2,1,0:T(2,128)}), f32[8,2,1024]{2,1,0:T(2,128)S(1)}, u32[]{:S(2)}, u32[]{:S(2)}) %all-to-all-start.5) | async-done | bytes 65568 | tf_op jit(solution)/shard_map/all_to_all | solution.py:13
  151.3 13.2 %while.109 = (s32[]{:T(128)}, f32[4,1,512]{2,1,0:T(1,128)S(1)}, f32[4,1,512]{2,1,0:T(1,128)S(1)}, s32[4]{0:T(128)S(1)}, bf16[1,2048,128]{2,1,0:T(8,128)(2,1)}, /...) while((s32[]{:T(128)}, f32[4,1,512]{2,1,0:T(1,128)S(1)}, ...), condition=%wide.region_27.28_spmd, body=%wide.region_24.27_spmd.sunk | while | flops 137886720 | bytes 4610223 | solution.py:130
  165.3 3.5 %all-to-all-start.6 = ((f32[16,2,2048]{2,1,0:T(2,128)}), f32[16,2,2048]{2,1,0:T(2,128)S(1)}, u32[]{:S(2)}, u32[]{:S(2)}) async-start(f32[16,2,2048]{2,1,0:T(2,128)} %broadcast_in_dim.90), calls=%async_computation.6 | async-start | bytes 524288 | tf_op jit(solution)/shard_map/all_to_all | solution.py:13
  168.9 9.9 %all-to-all-done.6 = f32[16,2,2048]{2,1,0:T(2,128)S(1)} async-done(((f32[16,2,2048]{2,1,0:T(2,128)}), f32[16,2,2048]{2,1,0:T(2,128)S(1)}, u32[]{:S(2)}, u32[]{:S(2)}) %all-to-all-start.6) | async-done | bytes 262176 | tf_op jit(solution)/shard_map/all_to_all | solution.py:13
  179.4 14.6 %while.110 = (s32[]{:T(128)}, bf16[4,1,512,128]{3,2,1,0:T(8,128)(2,1)}, s32[4]{0:T(128)S(1)}, bf16[1,2048,128]{2,1,0:T(8,128)(2,1)}, bf16[1,1024,128]{2,1,0:T(8,...) while((s32[]{:T(128)}, ...), condition=%wide.region_29.30_spmd, body=%wide.region_28.29_spmd.sunk | while | flops 270532608 | bytes 928439 | solution.py:167
  180.7 2.4 %fusion.112 = bf16[4,1,512,128]{3,2,1,0:T(8,128)(2,1)} fusion(bf16[4,1,512,128]{3,2,1,0:T(8,128)(2,1)} %get-tuple-element.1382, s32[]{:T(128)} %get-tuple-element.1381, f32[1024]{0:T(1024)S(1)} %bitcast.245, f32[512]{0:T(512)S(1)} %bitcast.271, bf16[1,1024,128]{2,1,0:T(8,128)(2,1)S(1)} %get-tuple-element.1400, ...), kind=kOutput, calls=%fused_computation.42.clone.1 | convolution fusion | flops 270532608 | bytes 924164 | tf_op jit(solution)/shard_map/while/body/eval_jaxpr/hqk,hkd->hqd/dot_general | solution.py:165
  184.3 2.4 %fusion.112 = bf16[4,1,512,128]{3,2,1,0:T(8,128)(2,1)} fusion(bf16[4,1,512,128]{3,2,1,0:T(8,128)(2,1)} %get-tuple-element.1382, s32[]{:T(128)} %get-tuple-element.1381, f32[1024]{0:T(1024)S(1)} %bitcast.245, f32[512]{0:T(512)S(1)} %bitcast.271, bf16[1,1024,128]{2,1,0:T(8,128)(2,1)S(1)} %get-tuple-element.1400, ...), kind=kOutput, calls=%fused_computation.42.clone.1 | convolution fusion | flops 270532608 | bytes 924164 | tf_op jit(solution)/shard_map/while/body/eval_jaxpr/hqk,hkd->hqd/dot_general | solution.py:165
  188.0 2.4 %fusion.112 = bf16[4,1,512,128]{3,2,1,0:T(8,128)(2,1)} fusion(bf16[4,1,512,128]{3,2,1,0:T(8,128)(2,1)} %get-tuple-element.1382, s32[]{:T(128)} %get-tuple-element.1381, f32[1024]{0:T(1024)S(1)} %bitcast.245, f32[512]{0:T(512)S(1)} %bitcast.271, bf16[1,1024,128]{2,1,0:T(8,128)(2,1)S(1)} %get-tuple-element.1400, ...), kind=kOutput, calls=%fused_computation.42.clone.1 | convolution fusion | flops 270532608 | bytes 924164 | tf_op jit(solution)/shard_map/while/body/eval_jaxpr/hqk,hkd->hqd/dot_general | solution.py:165
  191.6 2.4 %fusion.112 = bf16[4,1,512,128]{3,2,1,0:T(8,128)(2,1)} fusion(bf16[4,1,512,128]{3,2,1,0:T(8,128)(2,1)} %get-tuple-element.1382, s32[]{:T(128)} %get-tuple-element.1381, f32[1024]{0:T(1024)S(1)} %bitcast.245, f32[512]{0:T(512)S(1)} %bitcast.271, bf16[1,1024,128]{2,1,0:T(8,128)(2,1)S(1)} %get-tuple-element.1400, ...), kind=kOutput, calls=%fused_computation.42.clone.1 | convolution fusion | flops 270532608 | bytes 924164 | tf_op jit(solution)/shard_map/while/body/eval_jaxpr/hqk,hkd->hqd/dot_general | solution.py:165
  194.0 3.6 %all-to-all-start.7 = ((bf16[16,1,128,128]{3,2,1,0:T(8,128)(2,1)}), bf16[16,1,128,128]{3,2,1,0:T(8,128)(2,1)S(1)}, u32[]{:S(2)}, u32[]{:S(2)}) async-start(bf16[16,1,128,128]{3,2,1,0:T(8,128)(2,1)} %bitcast.45), calls=%async_computation.7 | async-start | bytes 1048576 | tf_op jit(solution)/shard_map/all_to_all | solution.py:74
  197.6 11.8 %all-to-all-done.7 = bf16[16,1,128,128]{3,2,1,0:T(8,128)(2,1)S(1)} async-done(((bf16[16,1,128,128]{3,2,1,0:T(8,128)(2,1)}), bf16[16,1,128,128]{3,2,1,0:T(8,128)(2,1)S(1)}, u32[]{:S(2)}, u32[]{:S(2)}) %all-to-all-start.7) | async-done | bytes 524320 | tf_op jit(solution)/shard_map/all_to_all | solution.py:74
  209.6 14.1 %all_to_all.45 = bf16[2,128,128]{1,2,0:T(8,128)(2,1)S(1)} all-to-all(bf16[2,128,128]{1,2,0:T(8,128)(2,1)S(1)} %broadcast_in_dim.91), channel_id=1, replica_groups=mesh['gz'=2,'gx'=8,'gy'=16] {'gz'}, dimensions={0} | all-to-all | bytes 131072 | tf_op jit(solution)/shard_map/all_to_all | solution.py:13
  (217 shorter events, 72.2 us)
Async XLA Ops:
  0.0 223.7 %copy-start = (bf16[256,2048]{1,0:T(8,128)(2,1)S(1)}, bf16[256,2048]{1,0:T(8,128)(2,1)}, u32[]{:S(2)}) copy-start(bf16[256,2048]{1,0:T(8,128)(2,1)} %param.23) | copy-start | bytes 3145732
  13.9 22.1 %copy-start.1 = (bf16[1,1024,128]{2,1,0:T(8,128)(2,1)S(1)}, bf16[1,1024,128]{2,1,0:T(8,128)(2,1)}, u32[]{:S(2)}) copy-start(bf16[1,1024,128]{2,1,0:T(8,128)(2,1)} %get-tuple-element.1405) | copy-start | bytes 786436
  14.7 20.6 %all-to-all-start = ((f32[16,2,2048]{2,1,0:T(2,128)}), f32[16,2,2048]{2,1,0:T(2,128)S(1)}, u32[]{:S(2)}, u32[]{:S(2)}) async-start(f32[16,2,2048]{2,1,0:T(2,128)} %broadcast_in_dim.84), calls=%async_computation | async-start | bytes 524288 | tf_op jit(solution)/shard_map/all_to_all | solution.py:13
  44.5 13.1 %all-to-all-start.1 = ((f32[8,2,1024]{2,1,0:T(2,128)}), f32[8,2,1024]{2,1,0:T(2,128)S(1)}, u32[]{:S(2)}, u32[]{:S(2)}) async-start(f32[8,2,1024]{2,1,0:T(2,128)} %broadcast_in_dim.85), calls=%async_computation.1 | async-start | bytes 131072 | tf_op jit(solution)/shard_map/all_to_all | solution.py:13
  71.7 13.4 %all-to-all-start.2 = ((f32[16,2,2048]{2,1,0:T(2,128)}), f32[16,2,2048]{2,1,0:T(2,128)S(1)}, u32[]{:S(2)}, u32[]{:S(2)}) async-start(f32[16,2,2048]{2,1,0:T(2,128)} %broadcast_in_dim.86), calls=%async_computation.2 | async-start | bytes 524288 | tf_op jit(solution)/shard_map/all_to_all | solution.py:13
  94.3 10.0 %all-to-all-start.3 = ((f32[8,2,1024]{2,1,0:T(2,128)}), f32[8,2,1024]{2,1,0:T(2,128)S(1)}, u32[]{:S(2)}, u32[]{:S(2)}) async-start(f32[8,2,1024]{2,1,0:T(2,128)} %broadcast_in_dim.87), calls=%async_computation.3 | async-start | bytes 131072 | tf_op jit(solution)/shard_map/all_to_all | solution.py:13
  118.5 13.4 %all-to-all-start.4 = ((f32[16,2,2048]{2,1,0:T(2,128)}), f32[16,2,2048]{2,1,0:T(2,128)S(1)}, u32[]{:S(2)}, u32[]{:S(2)}) async-start(f32[16,2,2048]{2,1,0:T(2,128)} %broadcast_in_dim.88), calls=%async_computation.4 | async-start | bytes 524288 | tf_op jit(solution)/shard_map/all_to_all | solution.py:13
  141.1 10.0 %all-to-all-start.5 = ((f32[8,2,1024]{2,1,0:T(2,128)}), f32[8,2,1024]{2,1,0:T(2,128)S(1)}, u32[]{:S(2)}, u32[]{:S(2)}) async-start(f32[8,2,1024]{2,1,0:T(2,128)} %broadcast_in_dim.89), calls=%async_computation.5 | async-start | bytes 131072 | tf_op jit(solution)/shard_map/all_to_all | solution.py:13
  164.5 14.9 %copy-start.2 = (bf16[1,1024,128]{2,1,0:T(8,128)(2,1)S(1)}, bf16[1,1024,128]{2,1,0:T(8,128)(2,1)}, u32[]{:S(2)}) copy-start(bf16[1,1024,128]{2,1,0:T(8,128)(2,1)} %param.22) | copy-start | bytes 786436
  165.3 13.4 %all-to-all-start.6 = ((f32[16,2,2048]{2,1,0:T(2,128)}), f32[16,2,2048]{2,1,0:T(2,128)S(1)}, u32[]{:S(2)}, u32[]{:S(2)}) async-start(f32[16,2,2048]{2,1,0:T(2,128)} %broadcast_in_dim.90), calls=%async_computation.6 | async-start | bytes 524288 | tf_op jit(solution)/shard_map/all_to_all | solution.py:13
  194.0 15.4 %all-to-all-start.7 = ((bf16[16,1,128,128]{3,2,1,0:T(8,128)(2,1)}), bf16[16,1,128,128]{3,2,1,0:T(8,128)(2,1)S(1)}, u32[]{:S(2)}, u32[]{:S(2)}) async-start(bf16[16,1,128,128]{3,2,1,0:T(8,128)(2,1)} %bitcast.45), calls=%async_computation.7 | async-start | bytes 1048576 | tf_op jit(solution)/shard_map/all_to_all | solution.py:74
where the time goes:
time: 226 us; the launch traced here: 225 us
  waiting for transfers between devices  72 us (32%)
  matrix products  50.1 us (22%)
  starting transfers between devices  37.3 us (17%)
  local copies, waits for them, and re-layouts  18.7 us (8%)
  other arithmetic  17.5 us (8%)
  loops' own time  14.4 us (6%)
  blocking collectives  14.1 us (6%)
    all_to_all x7, waiting for transfers between devices, copy_for_each(): return lax.all_to_all(copies, axis, split_axis=0, concat_axis=0, tiled=True)  60.1 us
    dot_general x28, matrix products, scores_at(): jnp.einsum('hqd,hkd->hqk', query_block, keys, preferred_element_type=jnp....  39.6 us
    all_to_all x7, starting transfers between devices, copy_for_each(): return lax.all_to_all(copies, axis, split_axis=0, concat_axis=0, tiled=True)  33.7 us
    all_to_all x1, blocking collectives, copy_for_each(): return lax.all_to_all(copies, axis, split_axis=0, concat_axis=0, tiled=True)  14.1 us
    dynamic_slice x20, local copies, waits for them, and re-layouts, row_step(): biggest, summed = lax.map(row_one_block, block_ids)  12 us
    all_to_all x1, waiting for transfers between devices, sum_at_owner(): tiles = lax.all_to_all(split_up(x, dim, size), axis, 0, 0, tiled=True)  11.8 us
    another operation x4, loops' own time, row_step(): biggest, summed = lax.map(row_one_block, block_ids)  10.9 us
    dot_general x4, matrix products, value_block(): jnp.einsum('hqk,hkd->hqd', weights, values, preferred_element_type=jnp.fl...  9.56 us
  transfers between devices with their start and end apart: 8, of which 8 were waited for; matrix products, arithmetic and copies ran while one was open for 0% of the time, Pallas kernels for 0%

commit v1 on v0

v1 whole, which is shorter than its diff:
```python
import functools
import math

import jax
import jax.numpy as jnp
from jax import lax
from jax.experimental import pallas as pl
from jax.experimental.pallas import tpu as pltpu
from jax.sharding import PartitionSpec as P

SWEEPS = 3
LANES = 128
MESH = pl.DeviceIdType.MESH
F32 = jnp.float32
BF16 = jnp.bfloat16


def far_first(count):
    return sorted(range(count), key=lambda d: -min(d, count - d))


def split_lhs(x):
    rows = jnp.broadcast_to(x, (16, x.shape[1]))
    hi = rows.astype(BF16).astype(F32)
    rest = rows - hi
    mid = rest.astype(BF16).astype(F32)
    lo = rest - mid
    at = lax.broadcasted_iota(jnp.int32, rows.shape, 0)
    parts = jnp.where(at == 0, hi, jnp.where(at == 1, mid, jnp.where(at == 2, lo, 0.0)))
    return parts.astype(BF16)


def kernel(
    sizes,
    q_hbm,
    k_hbm,
    v_hbm,
    w_hbm,
    out_ref,
    q_ref,
    k_ref,
    v_ref,
    w_ref,
    s_ref,
    f_ref,
    lhs_row,
    lhs_col,
    val_lhs,
    cmax_ref,
    row_send,
    row_recv,
    col_send,
    col_recv,
    row_vec,
    col_vec,
    out_send,
    out_recv,
    head_send,
    head_recv,
    load_sem,
    row_ssem,
    row_rsem,
    col_ssem,
    col_rsem,
    out_ssem,
    out_rsem,
    head_ssem,
    head_rsem,
):
    nx, ny = sizes
    rows, width = q_ref.shape
    cols = k_ref.shape[0]
    row_tiles, col_tiles = rows // LANES, cols // LANES
    nz = ny // 2
    gz, gx, gy = lax.axis_index("gz"), lax.axis_index("gx"), lax.axis_index("gy")
    z, xl = gy // 2, lax.rem(gy, 2)
    y, xh = gx // 2, lax.rem(gx, 2)
    scale = math.log2(math.e) / math.sqrt(width)

    row_peers = [(dz, dx) for dz in far_first(nz) for dx in (1, 0) if (dz, dx) != (0, 0)]
    col_peers = [(dy, dx) for dy in far_first(nx // 2) for dx in (1, 0) if (dy, dx) != (0, 0)]

    def row_peer(dz, dx):
        return lax.rem(z + dz, nz) * 2 + lax.rem(xl + dx, 2)

    def col_peer(dy, dx):
        return lax.rem(y + dy, nx // 2) * 2 + lax.rem(xh + dx, 2)

    mine = w_ref.shape[1]
    loads = [
        pltpu.make_async_copy(q_hbm, q_ref, load_sem.at[0]),
        pltpu.make_async_copy(k_hbm, k_ref, load_sem.at[1]),
        pltpu.make_async_copy(v_hbm, v_ref, load_sem.at[2]),
        pltpu.make_async_copy(
            w_hbm.at[:, pl.ds(pl.multiple_of(gz * mine, LANES), mine)], w_ref, load_sem.at[3]
        ),
    ]
    for load in loads:
        load.start()

    barrier = pltpu.get_barrier_semaphore()
    for dz, dx in row_peers:
        pl.semaphore_signal(
            barrier, inc=1, device_id={"gy": row_peer(dz, dx)}, device_id_type=MESH
        )
    for dy, dx in col_peers:
        pl.semaphore_signal(
            barrier, inc=1, device_id={"gx": col_peer(dy, dx)}, device_id_type=MESH
        )
    pl.semaphore_signal(barrier, inc=1, device_id={"gz": 1 - gz}, device_id_type=MESH)

    def send_rows(turn):
        copies = []
        for dz, dx in row_peers:
            slot = dz * 2 + dx
            copy = pltpu.make_async_remote_copy(
                src_ref=row_send.at[turn],
                dst_ref=row_recv.at[turn, slot],
                send_sem=row_ssem.at[turn, slot],
                recv_sem=row_rsem.at[turn, slot],
                device_id={"gy": row_peer(dz, dx)},
                device_id_type=MESH,
            )
            copy.start()
            copies.append((slot, copy))
        return copies

    def send_cols(turn):
        copies = []
        for dy, dx in col_peers:
            slot = dy * 2 + dx
            copy = pltpu.make_async_remote_copy(
                src_ref=col_send.at[turn],
                dst_ref=col_recv.at[turn, slot],
                send_sem=col_ssem.at[turn, slot],
                recv_sem=col_rsem.at[turn, slot],
                device_id={"gx": col_peer(dy, dx)},
                device_id_type=MESH,
            )
            copy.start()
            copies.append((slot, copy))
        return copies

    def log_total(own, received):
        biggest = own
        for other in received:
            biggest = jnp.maximum(biggest, other)
        total = jnp.exp2(own - biggest)
        for other in received:
            total = total + jnp.exp2(other - biggest)
        return biggest + jnp.log2(total)

    def plain_total(own, received):
        total = own
        for other in received:
            total = total + other
        return total

    started = []

    loads[0].wait()
    loads[1].wait()
    block = min(256, rows)
    for b in range(rows // block):
        lanes = slice(b * block, (b + 1) * block)
        scores = scale * lax.dot_general(
            k_ref[...], q_ref[lanes, :], (((1,), (1,)), ((), ())), preferred_element_type=F32
        )
        s_ref[:, lanes] = scores
        biggest = jnp.max(scores, axis=0, keepdims=True)
        summed = jnp.sum(jnp.exp2(s_ref[:, lanes] - biggest), axis=0, keepdims=True)
        local = biggest + jnp.log2(summed)
        for t in range(block // LANES):
            row_send[0, pl.ds(b * (block // LANES) + t, 1), :] = local[
                :, t * LANES : (t + 1) * LANES
            ]

    pl.semaphore_wait(barrier, len(row_peers) + len(col_peers) + 1)
    copies = send_rows(0)
    started += copies
    for _, copy in copies:
        copy.wait_recv()
    row_vec[...] = -log_total(row_send[0], [row_recv[0, slot] for slot, _ in copies])

    eye = lax.broadcasted_iota(jnp.int32, (LANES, LANES), 0) == lax.broadcasted_iota(
        jnp.int32, (LANES, LANES), 1
    )

    def across(column):
        return jnp.sum(
            jnp.where(eye, jnp.broadcast_to(column, (LANES, LANES)), 0.0), axis=0, keepdims=True
        )

    tiles = [slice(t * LANES, (t + 1) * LANES) for t in range(row_tiles)]
    for jb in range(col_tiles):
        down = slice(jb * LANES, (jb + 1) * LANES)
        biggest = s_ref[down, tiles[0]] + row_vec[0:1, :]
        for t in range(1, row_tiles):
            biggest = jnp.maximum(biggest, s_ref[down, tiles[t]] + row_vec[t : t + 1, :])
        biggest = jnp.max(biggest, axis=1, keepdims=True)
        wide = jnp.broadcast_to(biggest, (LANES, LANES))
        summed = jnp.zeros((LANES, LANES), F32)
        for t in range(row_tiles):
            part = jnp.exp2(s_ref[down, tiles[t]] + row_vec[t : t + 1, :] - wide)
            f_ref[down, tiles[t]] = part.astype(BF16)
            summed = summed + part
        summed = jnp.sum(summed, axis=1, keepdims=True)
        cmax_ref[pl.ds(jb, 1), :] = across(biggest)
        col_send[0, pl.ds(jb, 1), :] = across(biggest + jnp.log2(summed))

    copies = send_cols(0)
    started += copies
    loads[2].wait()
    loads[3].wait()
    for t in range(col_tiles):
        down = slice(t * LANES, (t + 1) * LANES)
        val_lhs[0:width, down] = v_ref[down, :].astype(F32).T.astype(BF16)
    for _, copy in copies:
        copy.wait_recv()
    total = log_total(col_send[0], [col_recv[0, slot] for slot, _ in copies])
    col_vec[...] = jnp.exp2(cmax_ref[...] - total)

    def row_step(turn):
        for t in range(col_tiles):
            lhs_row[:, t * LANES : (t + 1) * LANES] = split_lhs(col_vec[t : t + 1, :])
        sums = jnp.sum(
            lax.dot_general(
                lhs_row[...], f_ref[...], (((1,), (0,)), ((), ())), preferred_element_type=F32
            ),
            axis=0,
            keepdims=True,
        )
        for t in range(row_tiles):
            row_send[turn, pl.ds(t, 1), :] = sums[:, t * LANES : (t + 1) * LANES]
        copies = send_rows(turn)
        for _, copy in copies:
            copy.wait_recv()
        row_vec[...] = 1.0 / plain_total(
            row_send[turn], [row_recv[turn, slot] for slot, _ in copies]
        )
        return copies

    def col_step(turn):
        for t in range(row_tiles):
            lhs_col[:, t * LANES : (t + 1) * LANES] = split_lhs(row_vec[t : t + 1, :])
        sums = jnp.sum(
            lax.dot_general(
                lhs_col[...], f_ref[...], (((1,), (1,)), ((), ())), preferred_element_type=F32
            ),
            axis=0,
            keepdims=True,
        )
        for t in range(col_tiles):
            col_send[turn, pl.ds(t, 1), :] = (
                sums[:, t * LANES : (t + 1) * LANES] * col_vec[t : t + 1, :]
            )
        copies = send_cols(turn)
        for _, copy in copies:
            copy.wait_recv()
        col_vec[...] = col_vec[...] / plain_total(
            col_send[turn], [col_recv[turn, slot] for slot, _ in copies]
        )
        return copies

    for turn in range(1, SWEEPS):
        started += row_step(turn)
        started += col_step(turn)

    for t in range(col_tiles):
        down = slice(t * LANES, (t + 1) * LANES)
        val_lhs[0:width, down] = (val_lhs[0:width, down].astype(F32) * col_vec[t : t + 1, :]).astype(
            BF16
        )
        val_lhs[width : width + 16, down] = split_lhs(col_vec[t : t + 1, :])
    tail = lax.broadcasted_iota(jnp.int32, (16, LANES), 0)
    sends = []
    for dz in far_first(nz):
        there = lax.rem(z + dz, nz)
        part = jnp.dot(
            val_lhs[...],
            f_ref[:, pl.ds(pl.multiple_of(there * 2 * LANES, 2 * LANES), 2 * LANES)],
            preferred_element_type=F32,
        )
        for x in range(2):
            piece = part[:, x * LANES : (x + 1) * LANES]
            out_send[dz, x, 0:width, :] = piece[0:width].astype(BF16)
            weight = jnp.sum(piece[width:], axis=0, keepdims=True)
            high = weight.astype(BF16).astype(F32)
            out_send[dz, x, width : width + 16, :] = jnp.where(
                tail == 0, high, jnp.where(tail == 1, weight - high, 0.0)
            ).astype(BF16)
        for dx in (1, 0):
            if (dz, dx) != (0, 0):
                copy = pltpu.make_async_remote_copy(
                    src_ref=out_send.at[dz, lax.rem(xl + dx, 2)],
                    dst_ref=out_recv.at[dz, dx],
                    send_sem=out_ssem.at[dz, dx],
                    recv_sem=out_rsem.at[dz, dx],
                    device_id={"gy": row_peer(dz, dx)},
                    device_id_type=MESH,
                )
                copy.start()
                sends.append((dz, dx, copy))
    total = out_send[0, xl].astype(F32)
    for dz, dx, copy in reversed(sends):
        copy.wait_recv()
        total = total + out_recv[dz, dx].astype(F32)
    weight = jnp.sum(total[width:], axis=0, keepdims=True)
    head = (total[0:width] / weight).T.astype(BF16)
    head_send[...] = head
    swap = pltpu.make_async_remote_copy(
        src_ref=head_send,
        dst_ref=head_recv,
        send_sem=head_ssem,
        recv_sem=head_rsem,
        device_id={"gz": 1 - gz},
        device_id_type=MESH,
    )
    swap.start()

    def w_rows(which):
        return w_ref[pl.ds(pl.multiple_of(which * width, width), width), :]

    mixed = jnp.dot(head_send[...], w_rows(gz), preferred_element_type=F32)
    swap.wait_recv()
    mixed = mixed + jnp.dot(head_recv[...], w_rows(1 - gz), preferred_element_type=F32)
    out_ref[...] = mixed.astype(BF16)

    for _, copy in started:
        copy.wait_send()
    for _, _, copy in sends:
        copy.wait_send()
    swap.wait_send()


def solution(mesh):
    nx, ny = mesh.shape["gx"], mesh.shape["gy"]

    def body(queries, keys, values, w_out):
        _, rows, width = queries.shape
        cols = keys.shape[1]
        model = w_out.shape[1] // 2
        row_tiles, col_tiles = rows // LANES, cols // LANES
        anywhere = pl.BlockSpec(memory_space=pl.ANY)
        dma = pltpu.SemaphoreType.DMA
        return pl.pallas_call(
            functools.partial(kernel, (nx, ny)),
            out_shape=jax.ShapeDtypeStruct((rows // ny, model), BF16),
            in_specs=[anywhere] * 4,
            out_specs=pl.BlockSpec(memory_space=pltpu.VMEM),
            scratch_shapes=[
                pltpu.VMEM((rows, width), BF16),
                pltpu.VMEM((cols, width), BF16),
                pltpu.VMEM((cols, width), BF16),
                pltpu.VMEM((2 * width, model), BF16),
                pltpu.VMEM((cols, rows), F32),
                pltpu.VMEM((cols, rows), BF16),
                pltpu.VMEM((16, cols), BF16),
                pltpu.VMEM((16, rows), BF16),
                pltpu.VMEM((width + 16, cols), BF16),
                pltpu.VMEM((col_tiles, LANES), F32),
                pltpu.VMEM((SWEEPS, row_tiles, LANES), F32),
                pltpu.VMEM((SWEEPS, ny, row_tiles, LANES), F32),
                pltpu.VMEM((SWEEPS, col_tiles, LANES), F32),
                pltpu.VMEM((SWEEPS, nx, col_tiles, LANES), F32),
                pltpu.VMEM((row_tiles, LANES), F32),
                pltpu.VMEM((col_tiles, LANES), F32),
                pltpu.VMEM((ny // 2, 2, width + 16, LANES), BF16),
                pltpu.VMEM((ny // 2, 2, width + 16, LANES), BF16),
                pltpu.VMEM((LANES, width), BF16),
                pltpu.VMEM((LANES, width), BF16),
                dma((4,)),
                dma((SWEEPS, ny)),
                dma((SWEEPS, ny)),
                dma((SWEEPS, nx)),
                dma((SWEEPS, nx)),
                dma((ny // 2, 2)),
                dma((ny // 2, 2)),
                dma,
                dma,
            ],
            compiler_params=pltpu.CompilerParams(
                collective_id=0, has_side_effects=True, vmem_limit_bytes=56 * 1024 * 1024
            ),
        )(queries.reshape(rows, width), keys.reshape(cols, width), values.reshape(cols, width), w_out)

    return jax.shard_map(
        body,
        mesh=mesh,
        in_specs=(P("gz", "gx", None), P("gz", "gy", None), P("gz", "gy", None), P()),
        out_specs=P(("gx", "gy"), "gz"),
        check_vma=False,
    )
```

time: 226 us -> 64.2 us (0.28)
  waiting for transfers between devices: 72 us -> 0 us
  Pallas kernels: 0 us -> 62.4 us
  matrix products: 50.1 us -> 0 us
  starting transfers between devices: 37.3 us -> 0 us
  other arithmetic: 17.5 us -> 0 us
  local copies, waits for them, and re-layouts: 18.7 us -> 1.67 us
  loops' own time: 14.4 us -> 0 us
  blocking collectives: 14.1 us -> 0 us
    all_to_all x8 -> x0, waiting for transfers between devices: 72 us -> none  [the longest x7 60.1 us: copy_for_each(): return lax.all_to_all(copies, axis, split_axis=0, concat_axis=0, tiled=True)]
    pallas_call x0 -> x1, Pallas kernels: none -> 62.4 us  [body(): pl.pallas_call(functools.partial(kernel, (nx, ny)), out_shape=jax.ShapeDt...]
    dot_general x33 -> x0, matrix products: 50.1 us -> none  [the longest x28 39.6 us: scores_at(): jnp.einsum('hqd,hkd->hqk', query_block, keys, preferred_element_type=jnp....]
    all_to_all x8 -> x0, starting transfers between devices: 37.3 us -> none  [the longest x7 33.7 us: copy_for_each(): return lax.all_to_all(copies, axis, split_axis=0, concat_axis=0, tiled=True)]
    reduce_sum x29 -> x0, other arithmetic: 15.1 us -> none  [the longest x16 9.23 us: row_one_block(): summed = jnp.sum(jnp.exp(shifted - biggest[:, :, None]), axis=2)]
    another operation x8 -> x0, loops' own time: 14.4 us -> none  [the longest x4 10.9 us: row_step(): biggest, summed = lax.map(row_one_block, block_ids)]
    all_to_all x1 -> x0, blocking collectives: 14.1 us -> none  [copy_for_each(): return lax.all_to_all(copies, axis, split_axis=0, concat_axis=0, tiled=True)]
    dynamic_slice x36 -> x0, local copies, waits for them, and re-layouts: 12.1 us -> none  [the longest x20 12 us: row_step(): biggest, summed = lax.map(row_one_block, block_ids)]
  transfers between devices with their start and end apart: 8 -> 0, of which waited for: 8 -> 0; matrix products, arithmetic and copies ran while one was open for 0% -> 0% of each run, Pallas kernels for 0% -> 0%
where the time goes in v1:
time: 64.2 us; the launch traced here: 64.1 us
  Pallas kernels  62.4 us (97%)
  local copies, waits for them, and re-layouts  1.67 us (3%)
    pallas_call x1, Pallas kernels, body(): pl.pallas_call(functools.partial(kernel, (nx, ny)), out_shape=jax.ShapeDt...  62.4 us
    unnamed x1, local copies, waits for them, and re-layouts  1.67 us

profile of v1, /device:TPU:1, one launch (start us, length us, event | category | flops | bytes accessed | tf_op | source)
XLA Modules:
  0.0 64.1 jit_solution(7153749210093208312)
XLA Ops:
  0.0 62.4 %shard_map.46 = bf16[128,1024]{1,0:T(8,128)(2,1)} custom-call(bf16[2048,128]{1,0:T(8,128)(2,1)} %bitcast.3, bf16[1024,128]{1,0:T(8,128)(2,1)} %bitcast.4, bf16[1024,128]{1,0:T(8,128)(2,1)} %bitcast.5, bf16[256,2048]{1,0:T(8,128)(2,1)} %w_hbm.1), custom_call_target="tpu_custom_call" | custom-call | tf_op jit(solution)/shard_map/pallas_call | solution.py:346
  62.4 1.7 %copy.6 = bf16[128,1024]{1,0:T(8,128)(2,1)} copy(bf16[128,1024]{1,0:T(8,128)(2,1)} %shard_map.46) | data formatting | bytes 524288

commit v2 on v1

v2 whole, which is shorter than its diff:
```python
import functools
import math

import jax
import jax.numpy as jnp
from jax import lax
from jax.experimental import pallas as pl
from jax.experimental.pallas import tpu as pltpu
from jax.sharding import PartitionSpec as P

SWEEPS = 3
LANES = 128
MESH = pl.DeviceIdType.MESH
F32 = jnp.float32
BF16 = jnp.bfloat16


def far_first(count):
    return sorted(range(count), key=lambda d: -min(d, count - d))


def split_lhs(x):
    rows = jnp.broadcast_to(x, (16, x.shape[1]))
    hi = rows.astype(BF16).astype(F32)
    rest = rows - hi
    mid = rest.astype(BF16).astype(F32)
    lo = rest - mid
    at = lax.broadcasted_iota(jnp.int32, rows.shape, 0)
    parts = jnp.where(at == 0, hi, jnp.where(at == 1, mid, jnp.where(at == 2, lo, 0.0)))
    return parts.astype(BF16)


def kernel(
    sizes,
    q_hbm,
    k_hbm,
    v_hbm,
    out_ref,
    q_ref,
    k_ref,
    v_ref,
    k_parts,
    s_ref,
    f_ref,
    g_ref,
    lhs_row,
    lhs_col,
    val_lhs,
    cmax_ref,
    row_send,
    row_recv,
    sum_send,
    sum_recv,
    col_send,
    col_recv,
    row_vec,
    col_vec,
    out_send,
    out_recv,
    head_send,
    head_recv,
    load_sem,
    row_ssem,
    row_rsem,
    col_ssem,
    col_rsem,
    out_sem,
    head_sem,
):
    nx, ny = sizes
    rows, width = q_ref.shape
    cols = k_ref.shape[0]
    row_tiles, col_tiles = rows // LANES, cols // LANES
    nz = ny // 2
    gz, gx, gy = lax.axis_index("gz"), lax.axis_index("gx"), lax.axis_index("gy")
    z, xl = gy // 2, lax.rem(gy, 2)
    y, xh = gx // 2, lax.rem(gx, 2)
    scale = math.log2(math.e) / math.sqrt(width)

    row_peers = [(dz, dx) for dz in far_first(nz) for dx in (1, 0) if (dz, dx) != (0, 0)]
    col_peers = [(dy, dx) for dy in far_first(nx // 2) for dx in (1, 0) if (dy, dx) != (0, 0)]

    def row_peer(dz, dx):
        return lax.rem(z + dz, nz) * 2 + lax.rem(xl + dx, 2)

    def col_peer(dy, dx):
        return lax.rem(y + dy, nx // 2) * 2 + lax.rem(xh + dx, 2)

    loads = [
        pltpu.make_async_copy(q_hbm, q_ref, load_sem.at[0]),
        pltpu.make_async_copy(k_hbm, k_ref, load_sem.at[1]),
        pltpu.make_async_copy(v_hbm, v_ref, load_sem.at[2]),
    ]
    for load in loads:
        load.start()

    barrier = pltpu.get_barrier_semaphore()
    for dz, dx in row_peers:
        pl.semaphore_signal(
            barrier, inc=1, device_id={"gy": row_peer(dz, dx)}, device_id_type=MESH
        )
    for dy, dx in col_peers:
        pl.semaphore_signal(
            barrier, inc=1, device_id={"gx": col_peer(dy, dx)}, device_id_type=MESH
        )
    pl.semaphore_signal(barrier, inc=1, device_id={"gz": 1 - gz}, device_id_type=MESH)

    def send_all(source, target, ssem, rsem, peers):
        for slot, device in peers:
            pltpu.make_async_remote_copy(
                src_ref=source,
                dst_ref=target.at[slot],
                send_sem=ssem,
                recv_sem=rsem,
                device_id=device,
                device_id_type=MESH,
            ).start()

    def wait_all(target, sem):
        everything = target.at[pl.ds(1, target.shape[0] - 1)]
        pltpu.make_async_copy(everything, everything, sem).wait()

    row_to = [(dz * 2 + dx, {"gy": row_peer(dz, dx)}) for dz, dx in row_peers]
    col_to = [(dy * 2 + dx, {"gx": col_peer(dy, dx)}) for dy, dx in col_peers]

    def log_total(own, received):
        biggest = own
        for other in received:
            biggest = jnp.maximum(biggest, other)
        total = jnp.exp2(own - biggest)
        for other in received:
            total = total + jnp.exp2(other - biggest)
        return biggest + jnp.log2(total)

    def plain_total(own, received):
        total = own
        for other in received:
            total = total + other
        return total

    loads[1].wait()
    scaled = scale * k_ref[...].astype(F32)
    high = scaled.astype(BF16)
    k_parts[:, 0:width] = high
    k_parts[:, width:] = (scaled - high.astype(F32)).astype(BF16)
    loads[0].wait()
    block = 2 * LANES
    for b in range(rows // block):
        lanes = slice(b * block, (b + 1) * block)
        q_block = q_ref[lanes, :]
        scores = lax.dot_general(
            k_parts[...],
            jnp.concatenate([q_block, q_block], axis=1),
            (((1,), (1,)), ((), ())),
            preferred_element_type=F32,
        )
        s_ref[:, lanes] = scores
        biggest, summed = None, None
        for jb in range(col_tiles):
            part = scores[jb * LANES : (jb + 1) * LANES].reshape(LANES // 8, 8, block)
            top = jnp.max(part, axis=0)
            total = jnp.sum(jnp.exp2(part - top[None]), axis=0)
            if biggest is None:
                biggest, summed = top, total
            else:
                larger = jnp.maximum(biggest, top)
                summed = summed * jnp.exp2(biggest - larger) + total * jnp.exp2(top - larger)
                biggest = larger
        top = jnp.max(biggest, axis=0, keepdims=True)
        summed = jnp.sum(summed * jnp.exp2(biggest - top), axis=0, keepdims=True)
        local = top + jnp.log2(summed)
        for t in range(block // LANES):
            row_send[pl.ds(b * (block // LANES) + t, 1), :] = local[:, t * LANES : (t + 1) * LANES]

    pl.semaphore_wait(barrier, len(row_peers) + len(col_peers) + 1)
    send_all(row_send, row_recv, row_ssem.at[0], row_rsem.at[0], row_to)
    wait_all(row_recv, row_rsem.at[0])
    row_vec[...] = -log_total(row_send[...], [row_recv[slot] for slot in range(1, ny)])

    eye = lax.broadcasted_iota(jnp.int32, (LANES, LANES), 0) == lax.broadcasted_iota(
        jnp.int32, (LANES, LANES), 1
    )

    def across(column):
        return jnp.sum(
            jnp.where(eye, jnp.broadcast_to(column, (LANES, LANES)), 0.0), axis=0, keepdims=True
        )

    tiles = [slice(t * LANES, (t + 1) * LANES) for t in range(row_tiles)]
    for jb in range(col_tiles):
        down = slice(jb * LANES, (jb + 1) * LANES)
        biggest = None
        for t in range(row_tiles):
            shifted = s_ref[down, tiles[t]] + row_vec[t : t + 1, :]
            s_ref[down, tiles[t]] = shifted
            biggest = shifted if biggest is None else jnp.maximum(biggest, shifted)
        biggest = jnp.max(biggest, axis=1, keepdims=True)
        wide = jnp.broadcast_to(biggest, (LANES, LANES))
        summed = jnp.zeros((LANES, LANES), F32)
        for t in range(row_tiles):
            part = jnp.exp2(s_ref[down, tiles[t]] - wide)
            f_ref[down, tiles[t]] = part.astype(BF16)
            summed = summed + part
        summed = jnp.sum(summed, axis=1, keepdims=True)
        cmax_ref[pl.ds(jb, 1), :] = across(biggest)
        col_send[0, pl.ds(jb, 1), :] = across(biggest + jnp.log2(summed))

    send_all(col_send.at[0], col_recv.at[0], col_ssem.at[0], col_rsem.at[0], col_to)
    loads[2].wait()
    for t in range(col_tiles):
        down = slice(t * LANES, (t + 1) * LANES)
        val_lhs[0:width, down] = v_ref[down, :].astype(F32).T.astype(BF16)
        for i in range(row_tiles):
            g_ref[tiles[i], down] = f_ref[down, tiles[i]].T
    wait_all(col_recv.at[0], col_rsem.at[0])
    total = log_total(col_send[0], [col_recv[0, slot] for slot in range(1, nx)])
    col_vec[...] = jnp.exp2(cmax_ref[...] - total)

    def row_step(turn):
        for t in range(col_tiles):
            lhs_row[:, t * LANES : (t + 1) * LANES] = split_lhs(col_vec[t : t + 1, :])
        sums = jnp.sum(
            lax.dot_general(
                lhs_row[...], f_ref[...], (((1,), (0,)), ((), ())), preferred_element_type=F32
            ),
            axis=0,
            keepdims=True,
        )
        for t in range(row_tiles):
            row_vec[pl.ds(t, 1), :] = sums[:, t * LANES : (t + 1) * LANES]
        own = row_vec[...].astype(BF16)
        sum_send[turn - 1] = own
        send_all(
            sum_send.at[turn - 1], sum_recv.at[turn - 1], row_ssem.at[turn], row_rsem.at[turn], row_to
        )
        wait_all(sum_recv.at[turn - 1], row_rsem.at[turn])
        row_vec[...] = 1.0 / plain_total(
            own.astype(F32), [sum_recv[turn - 1, slot].astype(F32) for slot in range(1, ny)]
        )

    def col_step(turn):
        for t in range(row_tiles):
            lhs_col[:, t * LANES : (t + 1) * LANES] = split_lhs(row_vec[t : t + 1, :])
        sums = jnp.sum(
            lax.dot_general(
                lhs_col[...], g_ref[...], (((1,), (0,)), ((), ())), preferred_element_type=F32
            ),
            axis=0,
            keepdims=True,
        )
        for t in range(col_tiles):
            col_send[turn, pl.ds(t, 1), :] = (
                sums[:, t * LANES : (t + 1) * LANES] * col_vec[t : t + 1, :]
            )
        send_all(
            col_send.at[turn], col_recv.at[turn], col_ssem.at[turn], col_rsem.at[turn], col_to
        )
        wait_all(col_recv.at[turn], col_rsem.at[turn])
        col_vec[...] = col_vec[...] / plain_total(
            col_send[turn], [col_recv[turn, slot] for slot in range(1, nx)]
        )

    for turn in range(1, SWEEPS):
        row_step(turn)
        col_step(turn)

    for t in range(col_tiles):
        down = slice(t * LANES, (t + 1) * LANES)
        val_lhs[0:width, down] = (val_lhs[0:width, down].astype(F32) * col_vec[t : t + 1, :]).astype(
            BF16
        )
        val_lhs[width : width + 16, down] = split_lhs(col_vec[t : t + 1, :])
    tail = lax.broadcasted_iota(jnp.int32, (16, LANES), 0)

    def product(dz):
        there = lax.rem(z + dz, nz)
        return jnp.dot(
            val_lhs[...],
            f_ref[:, pl.ds(pl.multiple_of(there * 2 * LANES, 2 * LANES), 2 * LANES)],
            preferred_element_type=F32,
        )

    order = far_first(nz)
    ahead = product(order[0])
    for n, dz in enumerate(order):
        part = ahead
        if n + 1 < nz:
            ahead = product(order[n + 1])
        for x in range(2):
            piece = part[:, x * LANES : (x + 1) * LANES]
            out_send[dz, x, 0:width, :] = piece[0:width].astype(BF16)
            weight = jnp.sum(piece[width:], axis=0, keepdims=True)
            high = weight.astype(BF16).astype(F32)
            out_send[dz, x, width : width + 16, :] = jnp.where(
                tail == 0, high, jnp.where(tail == 1, weight - high, 0.0)
            ).astype(BF16)
        for dx in (1, 0):
            if (dz, dx) != (0, 0):
                pltpu.make_async_remote_copy(
                    src_ref=out_send.at[dz, lax.rem(xl + dx, 2)],
                    dst_ref=out_recv.at[dz * 2 + dx],
                    send_sem=out_sem.at[0],
                    recv_sem=out_sem.at[1],
                    device_id={"gy": row_peer(dz, dx)},
                    device_id_type=MESH,
                ).start()
    wait_all(out_recv, out_sem.at[1])
    total = out_send[0, xl].astype(F32)
    for slot in range(1, ny):
        total = total + out_recv[slot].astype(F32)
    weight = jnp.sum(total[width:], axis=0, keepdims=True)
    head = (total[0:width] / weight).T.astype(BF16)
    head_send[...] = head
    swap = pltpu.make_async_remote_copy(
        src_ref=head_send,
        dst_ref=head_recv,
        send_sem=head_sem.at[0],
        recv_sem=head_sem.at[1],
        device_id={"gz": 1 - gz},
        device_id_type=MESH,
    )
    swap.start()
    out_ref[:, pl.ds(pl.multiple_of(gz * width, width), width)] = head
    wait_all(row_recv, row_ssem.at[0])
    wait_all(col_recv.at[0], col_ssem.at[0])
    for turn in range(1, SWEEPS):
        wait_all(sum_recv.at[turn - 1], row_ssem.at[turn])
        wait_all(col_recv.at[turn], col_ssem.at[turn])
    wait_all(out_recv, out_sem.at[0])
    swap.wait()
    out_ref[:, pl.ds(pl.multiple_of((1 - gz) * width, width), width)] = head_recv[...]


def solution(mesh):
    nx, ny = mesh.shape["gx"], mesh.shape["gy"]

    def body(queries, keys, values, w_out):
        _, rows, width = queries.shape
        cols = keys.shape[1]
        columns = w_out.shape[1] // lax.axis_size("gz")
        row_tiles, col_tiles = rows // LANES, cols // LANES
        anywhere = pl.BlockSpec(memory_space=pl.ANY)
        dma = pltpu.SemaphoreType.DMA
        heads = pl.pallas_call(
            functools.partial(kernel, (nx, ny)),
            out_shape=jax.ShapeDtypeStruct((rows // ny, 2 * width), BF16),
            in_specs=[anywhere] * 3,
            out_specs=pl.BlockSpec(memory_space=pltpu.VMEM),
            scratch_shapes=[
                pltpu.VMEM((rows, width), BF16),
                pltpu.VMEM((cols, width), BF16),
                pltpu.VMEM((cols, width), BF16),
                pltpu.VMEM((cols, 2 * width), BF16),
                pltpu.VMEM((cols, rows), F32),
                pltpu.VMEM((cols, rows), BF16),
                pltpu.VMEM((rows, cols), BF16),
                pltpu.VMEM((16, cols), BF16),
                pltpu.VMEM((16, rows), BF16),
                pltpu.VMEM((width + 16, cols), BF16),
                pltpu.VMEM((col_tiles, LANES), F32),
                pltpu.VMEM((row_tiles, LANES), F32),
                pltpu.VMEM((ny, row_tiles, LANES), F32),
                pltpu.VMEM((SWEEPS - 1, row_tiles, LANES), BF16),
                pltpu.VMEM((SWEEPS - 1, ny, row_tiles, LANES), BF16),
                pltpu.VMEM((SWEEPS, col_tiles, LANES), F32),
                pltpu.VMEM((SWEEPS, nx, col_tiles, LANES), F32),
                pltpu.VMEM((row_tiles, LANES), F32),
                pltpu.VMEM((col_tiles, LANES), F32),
                pltpu.VMEM((ny // 2, 2, width + 16, LANES), BF16),
                pltpu.VMEM((ny, width + 16, LANES), BF16),
                pltpu.VMEM((LANES, width), BF16),
                pltpu.VMEM((LANES, width), BF16),
                dma((3,)),
                dma((SWEEPS,)),
                dma((SWEEPS,)),
                dma((SWEEPS,)),
                dma((SWEEPS,)),
                dma((2,)),
                dma((2,)),
            ],
            compiler_params=pltpu.CompilerParams(
                collective_id=0, has_side_effects=True, vmem_limit_bytes=56 * 1024 * 1024
            ),
        )(queries.reshape(rows, width), keys.reshape(cols, width), values.reshape(cols, width))
        w_columns = lax.dynamic_slice_in_dim(
            w_out, lax.axis_index("gz") * columns, columns, 1
        )
        return jnp.dot(heads, w_columns, preferred_element_type=F32).astype(BF16)

    return jax.shard_map(
        body,
        mesh=mesh,
        in_specs=(P("gz", "gx", None), P("gz", "gy", None), P("gz", "gy", None), P()),
        out_specs=P(("gx", "gy"), "gz"),
        check_vma=False,
    )
```

time: 64.2 us -> 60 us (0.935)
  Pallas kernels: 62.4 us -> 58 us
  matrix products: 0 us -> 1.79 us
  local copies, waits for them, and re-layouts: 1.67 us -> 0.01 us
    pallas_call x1, Pallas kernels: 62.4 us -> 58 us  [body(): pl.pallas_call(functools.partial(kernel, (nx, ny)), out_shape=jax.ShapeDt...]
    dot_general x0 -> x1, matrix products: none -> 1.79 us  [body(): return jnp.dot(heads, w_columns, preferred_element_type=F32).astype(BF16)]
    unnamed x1 -> x2, local copies, waits for them, and re-layouts: 1.67 us -> 0.01 us
where the time goes in v2:
time: 60 us; the launch traced here: 59.8 us
  Pallas kernels  58 us (97%)
  matrix products  1.79 us (3%)
    pallas_call x1, Pallas kernels, body(): pl.pallas_call(functools.partial(kernel, (nx, ny)), out_shape=jax.ShapeDt...  58 us
    dot_general x1, matrix products, body(): return jnp.dot(heads, w_columns, preferred_element_type=F32).astype(BF16)  1.79 us

profile of v2, /device:TPU:1, one launch (start us, length us, event | category | flops | bytes accessed | tf_op | source)
XLA Modules:
  0.0 59.8 jit_solution(1689292317638878293)
XLA Ops:
  0.0 0.0 copy-start
  0.0 58.0 %shard_map.46 = bf16[128,256]{1,0:T(8,128)(2,1)} custom-call(bf16[2048,128]{1,0:T(8,128)(2,1)} %bitcast.4, bf16[1024,128]{1,0:T(8,128)(2,1)} %bitcast.5, bf16[1024,128]{1,0:T(8,128)(2,1)} %bitcast.6), custom_call_target="tpu_custom_call" | custom-call | tf_op jit(solution)/shard_map/pallas_call | solution.py:344
  58.0 0.0 copy-done
  58.0 1.8 %convolution_convert_fusion = bf16[128,1024]{1,0:T(8,128)(2,1)} fusion(bf16[128,256]{1,0:T(8,128)(2,1)} %shard_map.46, bf16[256,2048]{1,0:T(8,128)(2,1)S(1)} %copy-done, s32[]{:T(128)S(6)} %select_n.3), kind=kOutput, calls=%fused_computation | convolution fusion | flops 67239936 | bytes 851972 | tf_op jit(solution)/shard_map/dot_general | solution.py:388
Async XLA Ops:
  0.0 58.0 %copy-start = (bf16[256,2048]{1,0:T(8,128)(2,1)S(1)}, bf16[256,2048]{1,0:T(8,128)(2,1)}, u32[]{:S(2)}) copy-start(bf16[256,2048]{1,0:T(8,128)(2,1)} %param.7) | copy-start | bytes 3145732

commit v3 on v2

--- a/solution.py
+++ b/solution.py
@@ -46,6 +46,16 @@
     lhs_row,
     lhs_col,
     val_lhs,
+    k2_ref,
+    v2_ref,
+    pair_ref,
+    wide_ref,
+    row_log,
+    log_send,
+    log_recv,
+    part_send,
+    part_recv,
+    side_recv,
     cmax_ref,
     row_send,
     row_recv,
@@ -66,6 +76,9 @@
     col_rsem,
     out_sem,
     head_sem,
+    pair_ssem,
+    pair_rsem,
+    side_sem,
 ):
     nx, ny = sizes
     rows, width = q_ref.shape
@@ -104,6 +117,14 @@
             barrier, inc=1, device_id={"gx": col_peer(dy, dx)}, device_id_type=MESH
         )
     pl.semaphore_signal(barrier, inc=1, device_id={"gz": 1 - gz}, device_id_type=MESH)
+    beside = z * 2 + 1 - xl
+    for dy, dx in col_peers:
+        pl.semaphore_signal(
+            barrier,
+            inc=1,
+            device_id={"gx": col_peer(dy, dx), "gy": beside},
+            device_id_type=MESH,
+        )
 
     def send_all(source, target, ssem, rsem, peers):
         for slot, device in peers:
@@ -122,6 +143,27 @@
 
     row_to = [(dz * 2 + dx, {"gy": row_peer(dz, dx)}) for dz, dx in row_peers]
     col_to = [(dy * 2 + dx, {"gx": col_peer(dy, dx)}) for dy, dx in col_peers]
+    side_to = [
+        (dy * 2 + dx, {"gx": col_peer(dy, dx), "gy": beside}) for dy, dx in [*col_peers, (0, 0)]
+    ]
+
+    def to_pair(source, target, number):
+        return pltpu.make_async_remote_copy(
+            src_ref=source,
+            dst_ref=target,
+            send_sem=pair_ssem.at[number],
+            recv_sem=pair_rsem.at[number],
+            device_id={"gy": beside},
+            device_id_type=MESH,
+        )
+
+    pair_copies = [
+        to_pair(k_ref, k2_ref, 0),
+        to_pair(v_ref, v2_ref, 1),
+        to_pair(log_send, log_recv, 2),
+        to_pair(part_send, part_recv, 3),
+    ]
+    order = far_first(nz)
 
     def log_total(own, received):
         biggest = own
@@ -172,10 +214,13 @@
         for t in range(block // LANES):
             row_send[pl.ds(b * (block // LANES) + t, 1), :] = local[:, t * LANES : (t + 1) * LANES]
 
-    pl.semaphore_wait(barrier, len(row_peers) + len(col_peers) + 1)
+    pl.semaphore_wait(barrier, len(row_peers) + 2 * len(col_peers) + 1)
     send_all(row_send, row_recv, row_ssem.at[0], row_rsem.at[0], row_to)
+    pair_copies[0].start()
     wait_all(row_recv, row_rsem.at[0])
-    row_vec[...] = -log_total(row_send[...], [row_recv[slot] for slot in range(1, ny)])
+    loads[2].wait()
+    pair_copies[1].start()
+    row_log[...] = -log_total(row_send[...], [row_recv[slot] for slot in range(1, ny)])
 
     eye = lax.broadcasted_iota(jnp.int32, (LANES, LANES), 0) == lax.broadcasted_iota(
         jnp.int32, (LANES, LANES), 1
@@ -191,7 +236,7 @@
         down = slice(jb * LANES, (jb + 1) * LANES)
         biggest = None
         for t in range(row_tiles):
-            shifted = s_ref[down, tiles[t]] + row_vec[t : t + 1, :]
+            shifted = s_ref[down, tiles[t]] + row_log[t : t + 1, :]
             s_ref[down, tiles[t]] = shifted
             biggest = shifted if biggest is None else jnp.maximum(biggest, shifted)
         biggest = jnp.max(biggest, axis=1, keepdims=True)
@@ -206,7 +251,6 @@
         col_send[0, pl.ds(jb, 1), :] = across(biggest + jnp.log2(summed))
 
     send_all(col_send.at[0], col_recv.at[0], col_ssem.at[0], col_rsem.at[0], col_to)
-    loads[2].wait()
     for t in range(col_tiles):
         down = slice(t * LANES, (t + 1) * LANES)
         val_lhs[0:width, down] = v_ref[down, :].astype(F32).T.astype(BF16)
@@ -214,7 +258,49 @@
             g_ref[tiles[i], down] = f_ref[down, tiles[i]].T
     wait_all(col_recv.at[0], col_rsem.at[0])
     total = log_total(col_send[0], [col_recv[0, slot] for slot in range(1, nx)])
+    log_send[...] = -total
+    pair_copies[2].start()
     col_vec[...] = jnp.exp2(cmax_ref[...] - total)
+
+    def for_pair():
+        pair_copies[0].wait_recv()
+        scaled = scale * k2_ref[...].astype(F32)
+        high = scaled.astype(BF16)
+        k_parts[:, 0:width] = high
+        k_parts[:, width:] = (scaled - high.astype(F32)).astype(BF16)
+        pair_copies[1].wait_recv()
+        for t in range(col_tiles):
+            down = slice(t * LANES, (t + 1) * LANES)
+            val_lhs[0:width, cols + t * LANES : cols + (t + 1) * LANES] = (
+                v2_ref[down, :].astype(F32).T.astype(BF16)
+            )
+        pair_copies[2].wait_recv()
+        for t in range(col_tiles):
+            line = jnp.broadcast_to(log_recv[t : t + 1, :], (LANES, LANES))
+            column = jnp.sum(jnp.where(eye, line, 0.0), axis=1, keepdims=True)
+            wide_ref[t * LANES : (t + 1) * LANES, :] = jnp.broadcast_to(column, (LANES, LANES))
+        for m in range(nz // 2):
+            chunks = [lax.rem(z + dz, nz) * 2 + xl for dz in order[2 * m : 2 * m + 2]]
+            q_block = jnp.concatenate(
+                [q_ref[pl.ds(pl.multiple_of(c * LANES, LANES), LANES), :] for c in chunks], axis=0
+            )
+            scores = lax.dot_general(
+                k_parts[...],
+                jnp.concatenate([q_block, q_block], axis=1),
+                (((1,), (1,)), ((), ())),
+                preferred_element_type=F32,
+            )
+            for n, c in enumerate(chunks):
+                across_lanes = slice((2 * m + n) * LANES, (2 * m + n + 1) * LANES)
+                part = scores[:, n * LANES : (n + 1) * LANES] + wide_ref[...]
+                pair_ref[cols:, across_lanes] = jnp.exp2(part + row_log[pl.ds(c, 1), :]).astype(BF16)
+
+    def own_half():
+        for n, dz in enumerate(order):
+            c = lax.rem(z + dz, nz) * 2 + xl
+            pair_ref[0:cols, n * LANES : (n + 1) * LANES] = f_ref[
+                :, pl.ds(pl.multiple_of(c * LANES, LANES), LANES)
+            ]
 
     def row_step(turn):
         for t in range(col_tiles):
@@ -233,6 +319,8 @@
         send_all(
             sum_send.at[turn - 1], sum_recv.at[turn - 1], row_ssem.at[turn], row_rsem.at[turn], row_to
         )
+        if turn == 1:
+            for_pair()
         wait_all(sum_recv.at[turn - 1], row_rsem.at[turn])
         row_vec[...] = 1.0 / plain_total(
             own.astype(F32), [sum_recv[turn - 1, slot].astype(F32) for slot in range(1, ny)]
@@ -255,58 +343,69 @@
         send_all(
             col_send.at[turn], col_recv.at[turn], col_ssem.at[turn], col_rsem.at[turn], col_to
         )
+        if turn == 1:
+            own_half()
+        if turn == SWEEPS - 1:
+            send_all(col_send.at[turn], side_recv, side_sem.at[0], side_sem.at[1], side_to)
         wait_all(col_recv.at[turn], col_rsem.at[turn])
-        col_vec[...] = col_vec[...] / plain_total(
+        inverse = 1.0 / plain_total(
             col_send[turn], [col_recv[turn, slot] for slot in range(1, nx)]
         )
+        col_vec[...] = col_vec[...] * inverse
+        if turn == 1:
+            part_send[...] = inverse
+            pair_copies[3].start()
 
     for turn in range(1, SWEEPS):
         row_step(turn)
         col_step(turn)
 
-    for t in range(col_tiles):
-        down = slice(t * LANES, (t + 1) * LANES)
-        val_lhs[0:width, down] = (val_lhs[0:width, down].astype(F32) * col_vec[t : t + 1, :]).astype(
-            BF16
-        )
-        val_lhs[width : width + 16, down] = split_lhs(col_vec[t : t + 1, :])
+    pltpu.make_async_copy(side_recv, side_recv, side_sem.at[1]).wait()
+    pair_copies[3].wait_recv()
+    side = part_recv[...] / plain_total(side_recv[0], [side_recv[slot] for slot in range(1, nx)])
+    for t in range(2 * col_tiles):
+        lanes = slice(t * LANES, (t + 1) * LANES)
+        if t < col_tiles:
+            line = col_vec[t : t + 1, :]
+        else:
+            line = side[t - col_tiles : t - col_tiles + 1, :]
+        val_lhs[0:width, lanes] = (val_lhs[0:width, lanes].astype(F32) * line).astype(BF16)
+        val_lhs[width : width + 16, lanes] = split_lhs(line)
     tail = lax.broadcasted_iota(jnp.int32, (16, LANES), 0)
 
-    def product(dz):
-        there = lax.rem(z + dz, nz)
+    def product(m):
         return jnp.dot(
             val_lhs[...],
-            f_ref[:, pl.ds(pl.multiple_of(there * 2 * LANES, 2 * LANES), 2 * LANES)],
+            pair_ref[:, m * 2 * LANES : (m + 1) * 2 * LANES],
             preferred_element_type=F32,
         )
 
-    order = far_first(nz)
-    ahead = product(order[0])
-    for n, dz in enumerate(order):
-        part = ahead
-        if n + 1 < nz:
-            ahead = product(order[n + 1])
+    ahead = product(0)
+    for m in range(nz // 2):
+        both = ahead
+        if m + 1 < nz // 2:
+            ahead = product(m + 1)
         for x in range(2):
-            piece = part[:, x * LANES : (x + 1) * LANES]
-            out_send[dz, x, 0:width, :] = piece[0:width].astype(BF16)
+            dz = order[2 * m + x]
+            piece = both[:, x * LANES : (x + 1) * LANES]
+            out_send[dz, 0:width, :] = piece[0:width].astype(BF16)
             weight = jnp.sum(piece[width:], axis=0, keepdims=True)
             high = weight.astype(BF16).astype(F32)
-            out_send[dz, x, width : width + 16, :] = jnp.where(
+            out_send[dz, width : width + 16, :] = jnp.where(
                 tail == 0, high, jnp.where(tail == 1, weight - high, 0.0)
             ).astype(BF16)
-        for dx in (1, 0):
-            if (dz, dx) != (0, 0):
+            if dz != 0:
                 pltpu.make_async_remote_copy(
-                    src_ref=out_send.at[dz, lax.rem(xl + dx, 2)],
-                    dst_ref=out_recv.at[dz * 2 + dx],
+                    src_ref=out_send.at[dz],
+                    dst_ref=out_recv.at[dz],
                     send_sem=out_sem.at[0],
                     recv_sem=out_sem.at[1],
-                    device_id={"gy": row_peer(dz, dx)},
+                    device_id={"gy": row_peer(dz, 0)},
                     device_id_type=MESH,
                 ).start()
     wait_all(out_recv, out_sem.at[1])
-    total = out_send[0, xl].astype(F32)
-    for slot in range(1, ny):
+    total = out_send[0].astype(F32)
+    for slot in range(1, nz):
         total = total + out_recv[slot].astype(F32)
     weight = jnp.sum(total[width:], axis=0, keepdims=True)
     head = (total[0:width] / weight).T.astype(BF16)
@@ -327,6 +426,9 @@
         wait_all(sum_recv.at[turn - 1], row_ssem.at[turn])
         wait_all(col_recv.at[turn], col_ssem.at[turn])
     wait_all(out_recv, out_sem.at[0])
+    pltpu.make_async_copy(side_recv, side_recv, side_sem.at[0]).wait()
+    for copy in pair_copies:
+        copy.wait_send()
     swap.wait()
     out_ref[:, pl.ds(pl.multiple_of((1 - gz) * width, width), width)] = head_recv[...]
 
@@ -356,7 +458,17 @@
                 pltpu.VMEM((rows, cols), BF16),
                 pltpu.VMEM((16, cols), BF16),
                 pltpu.VMEM((16, rows), BF16),
-                pltpu.VMEM((width + 16, cols), BF16),
+                pltpu.VMEM((width + 16, 2 * cols), BF16),
+                pltpu.VMEM((cols, width), BF16),
+                pltpu.VMEM((cols, width), BF16),
+                pltpu.VMEM((2 * cols, rows // 2), BF16),
+                pltpu.VMEM((cols, LANES), F32),
+                pltpu.VMEM((row_tiles, LANES), F32),
+                pltpu.VMEM((col_tiles, LANES), F32),
+                pltpu.VMEM((col_tiles, LANES), F32),
+                pltpu.VMEM((col_tiles, LANES), F32),
+                pltpu.VMEM((col_tiles, LANES), F32),
+                pltpu.VMEM((nx, col_tiles, LANES), F32),
                 pltpu.VMEM((col_tiles, LANES), F32),
                 pltpu.VMEM((row_tiles, LANES), F32),
                 pltpu.VMEM((ny, row_tiles, LANES), F32),
@@ -366,8 +478,8 @@
                 pltpu.VMEM((SWEEPS, nx, col_tiles, LANES), F32),
                 pltpu.VMEM((row_tiles, LANES), F32),
                 pltpu.VMEM((col_tiles, LANES), F32),
-                pltpu.VMEM((ny // 2, 2, width + 16, LANES), BF16),
-                pltpu.VMEM((ny, width + 16, LANES), BF16),
+                pltpu.VMEM((ny // 2, width + 16, LANES), BF16),
+                pltpu.VMEM((ny // 2, width + 16, LANES), BF16),
                 pltpu.VMEM((LANES, width), BF16),
                 pltpu.VMEM((LANES, width), BF16),
                 dma((3,)),
@@ -377,6 +489,9 @@
                 dma((SWEEPS,)),
                 dma((2,)),
                 dma((2,)),
+                dma((4,)),
+                dma((4,)),
+                dma((2,)),
             ],
             compiler_params=pltpu.CompilerParams(
                 collective_id=0, has_side_effects=True, vmem_limit_bytes=56 * 1024 * 1024

time: 60 us -> 61.2 us (1.020)
  Pallas kernels: 58 us -> 59.2 us
    pallas_call x1, Pallas kernels: 58 us -> 59.2 us  [body(): pl.pallas_call(functools.partial(kernel, (nx, ny)), out_shape=jax.ShapeDt...]
where the time goes in v3:
time: 61.2 us; the launch traced here: 61 us
  Pallas kernels  59.2 us (97%)
  matrix products  1.79 us (3%)
    pallas_call x1, Pallas kernels, body(): pl.pallas_call(functools.partial(kernel, (nx, ny)), out_shape=jax.ShapeDt...  59.2 us
    dot_general x1, matrix products, body(): return jnp.dot(heads, w_columns, preferred_element_type=F32).astype(BF16)  1.79 us

profile of v3, /device:TPU:1, one launch (start us, length us, event | category | flops | bytes accessed | tf_op | source)
XLA Modules:
  0.0 61.0 jit_solution(628373547600583829)
XLA Ops:
  0.0 0.0 copy-start
  0.0 59.2 %shard_map.46 = bf16[128,256]{1,0:T(8,128)(2,1)} custom-call(bf16[2048,128]{1,0:T(8,128)(2,1)} %bitcast.4, bf16[1024,128]{1,0:T(8,128)(2,1)} %bitcast.5, bf16[1024,128]{1,0:T(8,128)(2,1)} %bitcast.6), custom_call_target="tpu_custom_call" | custom-call | tf_op jit(solution)/shard_map/pallas_call | solution.py:446
  59.3 0.0 copy-done
  59.3 1.8 %convolution_convert_fusion = bf16[128,1024]{1,0:T(8,128)(2,1)} fusion(bf16[128,256]{1,0:T(8,128)(2,1)} %shard_map.46, bf16[256,2048]{1,0:T(8,128)(2,1)S(1)} %copy-done, s32[]{:T(128)S(6)} %select_n.3), kind=kOutput, calls=%fused_computation | convolution fusion | flops 67239936 | bytes 851972 | tf_op jit(solution)/shard_map/dot_general | solution.py:503
Async XLA Ops:
  0.0 59.3 %copy-start = (bf16[256,2048]{1,0:T(8,128)(2,1)S(1)}, bf16[256,2048]{1,0:T(8,128)(2,1)}, u32[]{:S(2)}) copy-start(bf16[256,2048]{1,0:T(8,128)(2,1)} %param.7) | copy-start | bytes 3145732

commit v4 on v3

--- a/solution.py
+++ b/solution.py
@@ -217,9 +217,9 @@
     pl.semaphore_wait(barrier, len(row_peers) + 2 * len(col_peers) + 1)
     send_all(row_send, row_recv, row_ssem.at[0], row_rsem.at[0], row_to)
     pair_copies[0].start()
-    wait_all(row_recv, row_rsem.at[0])
     loads[2].wait()
     pair_copies[1].start()
+    wait_all(row_recv, row_rsem.at[0])
     row_log[...] = -log_total(row_send[...], [row_recv[slot] for slot in range(1, ny)])
 
     eye = lax.broadcasted_iota(jnp.int32, (LANES, LANES), 0) == lax.broadcasted_iota(
@@ -441,7 +441,7 @@
         cols = keys.shape[1]
         columns = w_out.shape[1] // lax.axis_size("gz")
         row_tiles, col_tiles = rows // LANES, cols // LANES
-        anywhere = pl.BlockSpec(memory_space=pl.ANY)
+        anywhere = pl.BlockSpec(memory_space=pltpu.HBM)
         dma = pltpu.SemaphoreType.DMA
         heads = pl.pallas_call(
             functools.partial(kernel, (nx, ny)),
@@ -494,9 +494,9 @@
                 dma((2,)),
             ],
             compiler_params=pltpu.CompilerParams(
-                collective_id=0, has_side_effects=True, vmem_limit_bytes=56 * 1024 * 1024
+                collective_id=0, has_side_effects=True, vmem_limit_bytes=44 * 1024 * 1024
             ),
-        )(queries.reshape(rows, width), keys.reshape(cols, width), values.reshape(cols, width))
+        )(*(pltpu.with_memory_space_constraint(x, pltpu.HBM) for x in (queries.reshape(rows, width), keys.reshape(cols, width), values.reshape(cols, width))))
         w_columns = lax.dynamic_slice_in_dim(
             w_out, lax.axis_index("gz") * columns, columns, 1
         )

time: 61.2 us -> 59.7 us (0.975)
  matrix products: 1.79 us -> 0.95 us
    dot_general x1, matrix products: 1.79 us -> 0.95 us  [body(): return jnp.dot(heads, w_columns, preferred_element_type=F32).astype(BF16)]
where the time goes in v4:
time: 59.7 us; the launch traced here: 59.6 us
  Pallas kernels  58.6 us (98%)
  matrix products  0.95 us (2%)
    pallas_call x1, Pallas kernels, body(): pl.pallas_call(functools.partial(kernel, (nx, ny)), out_shape=jax.ShapeDt...  58.6 us

profile of v4, /device:TPU:1, one launch (start us, length us, event | category | flops | bytes accessed | tf_op | source)
XLA Modules:
  0.0 59.6 jit_solution(706161288350546533)
XLA Ops:
  0.0 0.0 copy-start
  0.0 58.6 %shard_map.46 = bf16[128,256]{1,0:T(8,128)(2,1)S(1)} custom-call(bf16[2048,128]{1,0:T(8,128)(2,1)} %bitcast.4, bf16[1024,128]{1,0:T(8,128)(2,1)} %bitcast.5, bf16[1024,128]{1,0:T(8,128)(2,1)} %bitcast.6), custom_call_target="tpu_custom_call" | custom-call | tf_op jit(solution)/shard_map/pallas_call | solution.py:446
  58.6 0.0 copy-done
  58.7 0.9 %convolution_convert_fusion = bf16[128,1024]{1,0:T(8,128)(2,1)} fusion(bf16[128,256]{1,0:T(8,128)(2,1)S(1)} %shard_map.46, bf16[256,2048]{1,0:T(8,128)(2,1)S(1)} %copy-done, s32[]{:T(128)S(6)} %select_n.3), kind=kOutput, calls=%fused_computation | convolution fusion | flops 67239936 | bytes 851972 | tf_op jit(solution)/shard_map/dot_general | solution.py:503
Async XLA Ops:
  0.0 58.6 %copy-start = (bf16[256,2048]{1,0:T(8,128)(2,1)S(1)}, bf16[256,2048]{1,0:T(8,128)(2,1)}, u32[]{:S(2)}) copy-start(bf16[256,2048]{1,0:T(8,128)(2,1)} %param.7) | copy-start | bytes 3145732

commit v5 on v4

--- a/solution.py
+++ b/solution.py
@@ -157,12 +157,12 @@
             device_id_type=MESH,
         )
 
-    pair_copies = [
-        to_pair(k_ref, k2_ref, 0),
-        to_pair(v_ref, v2_ref, 1),
-        to_pair(log_send, log_recv, 2),
-        to_pair(part_send, part_recv, 3),
-    ]
+    half = cols // 2
+    halves = [pl.ds(0, half), pl.ds(half, half)]
+    pair_keys = [to_pair(k_ref.at[h], k2_ref.at[h], n) for n, h in enumerate(halves)]
+    pair_values = [to_pair(v_ref.at[h], v2_ref.at[h], 2 + n) for n, h in enumerate(halves)]
+    pair_log = to_pair(log_send, log_recv, 4)
+    pair_part = to_pair(part_send, part_recv, 5)
     order = far_first(nz)
 
     def log_total(own, received):
@@ -216,9 +216,8 @@
 
     pl.semaphore_wait(barrier, len(row_peers) + 2 * len(col_peers) + 1)
     send_all(row_send, row_recv, row_ssem.at[0], row_rsem.at[0], row_to)
-    pair_copies[0].start()
+    pair_keys[0].start()
     loads[2].wait()
-    pair_copies[1].start()
     wait_all(row_recv, row_rsem.at[0])
     row_log[...] = -log_total(row_send[...], [row_recv[slot] for slot in range(1, ny)])
 
@@ -251,6 +250,7 @@
         col_send[0, pl.ds(jb, 1), :] = across(biggest + jnp.log2(summed))
 
     send_all(col_send.at[0], col_recv.at[0], col_ssem.at[0], col_rsem.at[0], col_to)
+    pair_keys[1].start()
     for t in range(col_tiles):
         down = slice(t * LANES, (t + 1) * LANES)
         val_lhs[0:width, down] = v_ref[down, :].astype(F32).T.astype(BF16)
@@ -259,22 +259,17 @@
     wait_all(col_recv.at[0], col_rsem.at[0])
     total = log_total(col_send[0], [col_recv[0, slot] for slot in range(1, nx)])
     log_send[...] = -total
-    pair_copies[2].start()
+    pair_log.start()
     col_vec[...] = jnp.exp2(cmax_ref[...] - total)
 
     def for_pair():
-        pair_copies[0].wait_recv()
+        pair_keys[0].wait_recv()
+        pair_keys[1].wait_recv()
         scaled = scale * k2_ref[...].astype(F32)
         high = scaled.astype(BF16)
         k_parts[:, 0:width] = high
         k_parts[:, width:] = (scaled - high.astype(F32)).astype(BF16)
-        pair_copies[1].wait_recv()
-        for t in range(col_tiles):
-            down = slice(t * LANES, (t + 1) * LANES)
-            val_lhs[0:width, cols + t * LANES : cols + (t + 1) * LANES] = (
-                v2_ref[down, :].astype(F32).T.astype(BF16)
-            )
-        pair_copies[2].wait_recv()
+        pair_log.wait_recv()
         for t in range(col_tiles):
             line = jnp.broadcast_to(log_recv[t : t + 1, :], (LANES, LANES))
             column = jnp.sum(jnp.where(eye, line, 0.0), axis=1, keepdims=True)
@@ -295,6 +290,15 @@
                 part = scores[:, n * LANES : (n + 1) * LANES] + wide_ref[...]
                 pair_ref[cols:, across_lanes] = jnp.exp2(part + row_log[pl.ds(c, 1), :]).astype(BF16)
 
+    def values_of_pair():
+        pair_values[0].wait_recv()
+        pair_values[1].wait_recv()
+        for t in range(col_tiles):
+            down = slice(t * LANES, (t + 1) * LANES)
+            val_lhs[0:width, cols + t * LANES : cols + (t + 1) * LANES] = (
+                v2_ref[down, :].astype(F32).T.astype(BF16)
+            )
+
     def own_half():
         for n, dz in enumerate(order):
             c = lax.rem(z + dz, nz) * 2 + xl
@@ -320,7 +324,10 @@
             sum_send.at[turn - 1], sum_recv.at[turn - 1], row_ssem.at[turn], row_rsem.at[turn], row_to
         )
         if turn == 1:
+            pair_values[0].start()
             for_pair()
+        else:
+            values_of_pair()
         wait_all(sum_recv.at[turn - 1], row_rsem.at[turn])
         row_vec[...] = 1.0 / plain_total(
             own.astype(F32), [sum_recv[turn - 1, slot].astype(F32) for slot in range(1, ny)]
@@ -344,6 +351,7 @@
             col_send.at[turn], col_recv.at[turn], col_ssem.at[turn], col_rsem.at[turn], col_to
         )
         if turn == 1:
+            pair_values[1].start()
             own_half()
         if turn == SWEEPS - 1:
             send_all(col_send.at[turn], side_recv, side_sem.at[0], side_sem.at[1], side_to)
@@ -354,14 +362,14 @@
         col_vec[...] = col_vec[...] * inverse
         if turn == 1:
             part_send[...] = inverse
-            pair_copies[3].start()
+            pair_part.start()
 
     for turn in range(1, SWEEPS):
         row_step(turn)
         col_step(turn)
 
     pltpu.make_async_copy(side_recv, side_recv, side_sem.at[1]).wait()
-    pair_copies[3].wait_recv()
+    pair_part.wait_recv()
     side = part_recv[...] / plain_total(side_recv[0], [side_recv[slot] for slot in range(1, nx)])
     for t in range(2 * col_tiles):
         lanes = slice(t * LANES, (t + 1) * LANES)
@@ -427,7 +435,7 @@
         wait_all(col_recv.at[turn], col_ssem.at[turn])
     wait_all(out_recv, out_sem.at[0])
     pltpu.make_async_copy(side_recv, side_recv, side_sem.at[0]).wait()
-    for copy in pair_copies:
+    for copy in [*pair_keys, *pair_values, pair_log, pair_part]:
         copy.wait_send()
     swap.wait()
     out_ref[:, pl.ds(pl.multiple_of((1 - gz) * width, width), width)] = head_recv[...]
@@ -489,14 +497,19 @@
                 dma((SWEEPS,)),
                 dma((2,)),
                 dma((2,)),
-                dma((4,)),
-                dma((4,)),
+                dma((6,)),
+                dma((6,)),
                 dma((2,)),
             ],
             compiler_params=pltpu.CompilerParams(
                 collective_id=0, has_side_effects=True, vmem_limit_bytes=44 * 1024 * 1024
             ),
-        )(*(pltpu.with_memory_space_constraint(x, pltpu.HBM) for x in (queries.reshape(rows, width), keys.reshape(cols, width), values.reshape(cols, width))))
+        )(
+            *(
+                pltpu.with_memory_space_constraint(x.reshape(-1, width), pltpu.HBM)
+                for x in (queries, keys, values)
+            )
+        )
         w_columns = lax.dynamic_slice_in_dim(
             w_out, lax.axis_index("gz") * columns, columns, 1
         )

time: 59.7 us -> 55.5 us (0.930)
  Pallas kernels: 58.6 us -> 54.4 us
    pallas_call x1, Pallas kernels: 58.6 us -> 54.4 us  [body(): pl.pallas_call(functools.partial(kernel, (nx, ny)), out_shape=jax.ShapeDt...]
where the time goes in v5:
time: 55.5 us; the launch traced here: 55.4 us
  Pallas kernels  54.4 us (98%)
  matrix products  0.95 us (2%)
    pallas_call x1, Pallas kernels, body(): pl.pallas_call(functools.partial(kernel, (nx, ny)), out_shape=jax.ShapeDt...  54.4 us

profile of v5, /device:TPU:1, one launch (start us, length us, event | category | flops | bytes accessed | tf_op | source)
XLA Modules:
  0.0 55.4 jit_solution(9476316358914911575)
XLA Ops:
  0.0 0.0 copy-start
  0.0 54.4 %shard_map.46 = bf16[128,256]{1,0:T(8,128)(2,1)S(1)} custom-call(bf16[2048,128]{1,0:T(8,128)(2,1)} %bitcast.4, bf16[1024,128]{1,0:T(8,128)(2,1)} %bitcast.5, bf16[1024,128]{1,0:T(8,128)(2,1)} %bitcast.6), custom_call_target="tpu_custom_call" | custom-call | tf_op jit(solution)/shard_map/pallas_call | solution.py:454
  54.4 0.0 copy-done
  54.5 0.9 %convolution_convert_fusion = bf16[128,1024]{1,0:T(8,128)(2,1)} fusion(bf16[128,256]{1,0:T(8,128)(2,1)S(1)} %shard_map.46, bf16[256,2048]{1,0:T(8,128)(2,1)S(1)} %copy-done, s32[]{:T(128)S(6)} %select_n.3), kind=kOutput, calls=%fused_computation | convolution fusion | flops 67239936 | bytes 851972 | tf_op jit(solution)/shard_map/dot_general | solution.py:516
Async XLA Ops:
  0.0 54.4 %copy-start = (bf16[256,2048]{1,0:T(8,128)(2,1)S(1)}, bf16[256,2048]{1,0:T(8,128)(2,1)}, u32[]{:S(2)}) copy-start(bf16[256,2048]{1,0:T(8,128)(2,1)} %param.7) | copy-start | bytes 3145732

commit v6 on v5

--- a/solution.py
+++ b/solution.py
@@ -101,11 +101,13 @@
 
     loads = [
         pltpu.make_async_copy(q_hbm, q_ref, load_sem.at[0]),
-        pltpu.make_async_copy(k_hbm, k_ref, load_sem.at[1]),
+        pltpu.make_async_copy(k_hbm, k_parts.at[:, pl.ds(0, width)], load_sem.at[1]),
         pltpu.make_async_copy(v_hbm, v_ref, load_sem.at[2]),
+        pltpu.make_async_copy(k_hbm, k_parts.at[:, pl.ds(width, width)], load_sem.at[3]),
+        pltpu.make_async_copy(k_hbm, k_ref, load_sem.at[4]),
     ]
-    for load in loads:
-        load.start()
+    for n in (1, 3, 0, 4, 2):
+        loads[n].start()
 
     barrier = pltpu.get_barrier_semaphore()
     for dz, dx in row_peers:
@@ -163,7 +165,11 @@
     pair_values = [to_pair(v_ref.at[h], v2_ref.at[h], 2 + n) for n, h in enumerate(halves)]
     pair_log = to_pair(log_send, log_recv, 4)
     pair_part = to_pair(part_send, part_recv, 5)
-    order = far_first(nz)
+
+    def ranked(n):
+        return jnp.where(n < nz // 2, n, nz + nz // 2 - 1 - n)
+
+    targets = [ranked(jnp.where(n >= ranked(z), n + 1, n)) for n in range(nz - 1)] + [z]
 
     def log_total(own, received):
         biggest = own
@@ -181,18 +187,20 @@
         return total
 
     loads[1].wait()
-    scaled = scale * k_ref[...].astype(F32)
-    high = scaled.astype(BF16)
-    k_parts[:, 0:width] = high
-    k_parts[:, width:] = (scaled - high.astype(F32)).astype(BF16)
+    loads[3].wait()
     loads[0].wait()
+
+    def scaled_parts(x):
+        scaled = scale * x.astype(F32)
+        high = scaled.astype(BF16)
+        return jnp.concatenate([high, (scaled - high.astype(F32)).astype(BF16)], axis=1)
+
     block = 2 * LANES
     for b in range(rows // block):
         lanes = slice(b * block, (b + 1) * block)
-        q_block = q_ref[lanes, :]
         scores = lax.dot_general(
             k_parts[...],
-            jnp.concatenate([q_block, q_block], axis=1),
+            scaled_parts(q_ref[lanes, :]),
             (((1,), (1,)), ((), ())),
             preferred_element_type=F32,
         )
@@ -216,6 +224,7 @@
 
     pl.semaphore_wait(barrier, len(row_peers) + 2 * len(col_peers) + 1)
     send_all(row_send, row_recv, row_ssem.at[0], row_rsem.at[0], row_to)
+    loads[4].wait()
     pair_keys[0].start()
     loads[2].wait()
     wait_all(row_recv, row_rsem.at[0])
@@ -265,23 +274,21 @@
     def for_pair():
         pair_keys[0].wait_recv()
         pair_keys[1].wait_recv()
-        scaled = scale * k2_ref[...].astype(F32)
-        high = scaled.astype(BF16)
-        k_parts[:, 0:width] = high
-        k_parts[:, width:] = (scaled - high.astype(F32)).astype(BF16)
+        k_parts[:, 0:width] = k2_ref[...]
+        k_parts[:, width:] = k2_ref[...]
         pair_log.wait_recv()
         for t in range(col_tiles):
             line = jnp.broadcast_to(log_recv[t : t + 1, :], (LANES, LANES))
             column = jnp.sum(jnp.where(eye, line, 0.0), axis=1, keepdims=True)
             wide_ref[t * LANES : (t + 1) * LANES, :] = jnp.broadcast_to(column, (LANES, LANES))
         for m in range(nz // 2):
-            chunks = [lax.rem(z + dz, nz) * 2 + xl for dz in order[2 * m : 2 * m + 2]]
+            chunks = [to * 2 + xl for to in targets[2 * m : 2 * m + 2]]
             q_block = jnp.concatenate(
                 [q_ref[pl.ds(pl.multiple_of(c * LANES, LANES), LANES), :] for c in chunks], axis=0
             )
             scores = lax.dot_general(
                 k_parts[...],
-                jnp.concatenate([q_block, q_block], axis=1),
+                scaled_parts(q_block),
                 (((1,), (1,)), ((), ())),
                 preferred_element_type=F32,
             )
@@ -300,8 +307,8 @@
             )
 
     def own_half():
-        for n, dz in enumerate(order):
-            c = lax.rem(z + dz, nz) * 2 + xl
+        for n, to in enumerate(targets):
+            c = to * 2 + xl
             pair_ref[0:cols, n * LANES : (n + 1) * LANES] = f_ref[
                 :, pl.ds(pl.multiple_of(c * LANES, LANES), LANES)
             ]
@@ -394,25 +401,25 @@
         if m + 1 < nz // 2:
             ahead = product(m + 1)
         for x in range(2):
-            dz = order[2 * m + x]
+            n = 2 * m + x
             piece = both[:, x * LANES : (x + 1) * LANES]
-            out_send[dz, 0:width, :] = piece[0:width].astype(BF16)
+            out_send[n, 0:width, :] = piece[0:width].astype(BF16)
             weight = jnp.sum(piece[width:], axis=0, keepdims=True)
             high = weight.astype(BF16).astype(F32)
-            out_send[dz, width : width + 16, :] = jnp.where(
+            out_send[n, width : width + 16, :] = jnp.where(
                 tail == 0, high, jnp.where(tail == 1, weight - high, 0.0)
             ).astype(BF16)
-            if dz != 0:
+            if n != nz - 1:
                 pltpu.make_async_remote_copy(
-                    src_ref=out_send.at[dz],
-                    dst_ref=out_recv.at[dz],
+                    src_ref=out_send.at[n],
+                    dst_ref=out_recv.at[lax.rem(z - targets[n] + nz, nz)],
                     send_sem=out_sem.at[0],
                     recv_sem=out_sem.at[1],
-                    device_id={"gy": row_peer(dz, 0)},
+                    device_id={"gy": targets[n] * 2 + xl},
                     device_id_type=MESH,
                 ).start()
     wait_all(out_recv, out_sem.at[1])
-    total = out_send[0].astype(F32)
+    total = out_send[nz - 1].astype(F32)
     for slot in range(1, nz):
         total = total + out_recv[slot].astype(F32)
     weight = jnp.sum(total[width:], axis=0, keepdims=True)
@@ -490,7 +497,7 @@
                 pltpu.VMEM((ny // 2, width + 16, LANES), BF16),
                 pltpu.VMEM((LANES, width), BF16),
                 pltpu.VMEM((LANES, width), BF16),
-                dma((3,)),
+                dma((5,)),
                 dma((SWEEPS,)),
                 dma((SWEEPS,)),
                 dma((SWEEPS,)),

time: 55.5 us -> 54.2 us (0.977)
  Pallas kernels: 54.4 us -> 53.2 us
    pallas_call x1, Pallas kernels: 54.4 us -> 53.2 us  [body(): pl.pallas_call(functools.partial(kernel, (nx, ny)), out_shape=jax.ShapeDt...]
where the time goes in v6:
time: 54.2 us; the launch traced here: 54.1 us
  Pallas kernels  53.2 us (98%)
  matrix products  0.95 us (2%)
    pallas_call x1, Pallas kernels, body(): pl.pallas_call(functools.partial(kernel, (nx, ny)), out_shape=jax.ShapeDt...  53.2 us

profile of v6, /device:TPU:1, one launch (start us, length us, event | category | flops | bytes accessed | tf_op | source)
XLA Modules:
  0.0 54.1 jit_solution(17500295497382606140)
XLA Ops:
  0.0 0.0 copy-start
  0.0 53.2 %shard_map.46 = bf16[128,256]{1,0:T(8,128)(2,1)S(1)} custom-call(bf16[2048,128]{1,0:T(8,128)(2,1)} %bitcast.4, bf16[1024,128]{1,0:T(8,128)(2,1)} %bitcast.5, bf16[1024,128]{1,0:T(8,128)(2,1)} %bitcast.6), custom_call_target="tpu_custom_call" | custom-call | tf_op jit(solution)/shard_map/pallas_call | solution.py:461
  53.2 0.0 copy-done
  53.2 0.9 %convolution_convert_fusion = bf16[128,1024]{1,0:T(8,128)(2,1)} fusion(bf16[128,256]{1,0:T(8,128)(2,1)S(1)} %shard_map.46, bf16[256,2048]{1,0:T(8,128)(2,1)S(1)} %copy-done, s32[]{:T(128)S(6)} %select_n.3), kind=kOutput, calls=%fused_computation | convolution fusion | flops 67239936 | bytes 851972 | tf_op jit(solution)/shard_map/dot_general | solution.py:523
Async XLA Ops:
  0.0 53.2 %copy-start = (bf16[256,2048]{1,0:T(8,128)(2,1)S(1)}, bf16[256,2048]{1,0:T(8,128)(2,1)}, u32[]{:S(2)}) copy-start(bf16[256,2048]{1,0:T(8,128)(2,1)} %param.7) | copy-start | bytes 3145732

commit v7 on v6

--- a/solution.py
+++ b/solution.py
@@ -70,6 +70,7 @@
     head_send,
     head_recv,
     load_sem,
+    first_sem,
     row_ssem,
     row_rsem,
     col_ssem,
@@ -195,6 +196,15 @@
         high = scaled.astype(BF16)
         return jnp.concatenate([high, (scaled - high.astype(F32)).astype(BF16)], axis=1)
 
+    def send_rows(side_of):
+        send_all(
+            row_send.at[side_of],
+            row_recv.at[side_of],
+            first_sem.at[2 + side_of],
+            first_sem.at[side_of],
+            row_to,
+        )
+
     block = 2 * LANES
     for b in range(rows // block):
         lanes = slice(b * block, (b + 1) * block)
@@ -205,30 +215,33 @@
             preferred_element_type=F32,
         )
         s_ref[:, lanes] = scores
-        biggest, summed = None, None
+        tops, sums = [], []
         for jb in range(col_tiles):
             part = scores[jb * LANES : (jb + 1) * LANES].reshape(LANES // 8, 8, block)
             top = jnp.max(part, axis=0)
-            total = jnp.sum(jnp.exp2(part - top[None]), axis=0)
-            if biggest is None:
-                biggest, summed = top, total
-            else:
-                larger = jnp.maximum(biggest, top)
-                summed = summed * jnp.exp2(biggest - larger) + total * jnp.exp2(top - larger)
-                biggest = larger
+            tops.append(top)
+            sums.append(jnp.sum(jnp.exp2(part - top[None]), axis=0))
+        biggest = functools.reduce(jnp.maximum, tops)
+        summed = sum(total * jnp.exp2(top - biggest) for top, total in zip(tops, sums))
         top = jnp.max(biggest, axis=0, keepdims=True)
         summed = jnp.sum(summed * jnp.exp2(biggest - top), axis=0, keepdims=True)
         local = top + jnp.log2(summed)
         for t in range(block // LANES):
-            row_send[pl.ds(b * (block // LANES) + t, 1), :] = local[:, t * LANES : (t + 1) * LANES]
-
-    pl.semaphore_wait(barrier, len(row_peers) + 2 * len(col_peers) + 1)
-    send_all(row_send, row_recv, row_ssem.at[0], row_rsem.at[0], row_to)
+            side_of, line = divmod(b * (block // LANES) + t, row_tiles // 2)
+            row_send[side_of, pl.ds(line, 1), :] = local[:, t * LANES : (t + 1) * LANES]
+        if b + 1 == rows // block // 2:
+            pl.semaphore_wait(barrier, len(row_peers) + 2 * len(col_peers) + 1)
+            send_rows(0)
+
+    send_rows(1)
     loads[4].wait()
     pair_keys[0].start()
     loads[2].wait()
-    wait_all(row_recv, row_rsem.at[0])
-    row_log[...] = -log_total(row_send[...], [row_recv[slot] for slot in range(1, ny)])
+    for side_of in range(2):
+        wait_all(row_recv.at[side_of], first_sem.at[side_of])
+        row_log[side_of * (row_tiles // 2) : (side_of + 1) * (row_tiles // 2), :] = -log_total(
+            row_send[side_of], [row_recv[side_of, slot] for slot in range(1, ny)]
+        )
 
     eye = lax.broadcasted_iota(jnp.int32, (LANES, LANES), 0) == lax.broadcasted_iota(
         jnp.int32, (LANES, LANES), 1
@@ -328,14 +341,14 @@
         own = row_vec[...].astype(BF16)
         sum_send[turn - 1] = own
         send_all(
-            sum_send.at[turn - 1], sum_recv.at[turn - 1], row_ssem.at[turn], row_rsem.at[turn], row_to
+            sum_send.at[turn - 1], sum_recv.at[turn - 1], row_ssem.at[turn - 1], row_rsem.at[turn - 1], row_to
         )
         if turn == 1:
             pair_values[0].start()
             for_pair()
         else:
             values_of_pair()
-        wait_all(sum_recv.at[turn - 1], row_rsem.at[turn])
+        wait_all(sum_recv.at[turn - 1], row_rsem.at[turn - 1])
         row_vec[...] = 1.0 / plain_total(
             own.astype(F32), [sum_recv[turn - 1, slot].astype(F32) for slot in range(1, ny)]
         )
@@ -435,10 +448,11 @@
     )
     swap.start()
     out_ref[:, pl.ds(pl.multiple_of(gz * width, width), width)] = head
-    wait_all(row_recv, row_ssem.at[0])
+    for side_of in range(2):
+        wait_all(row_recv.at[side_of], first_sem.at[2 + side_of])
     wait_all(col_recv.at[0], col_ssem.at[0])
     for turn in range(1, SWEEPS):
-        wait_all(sum_recv.at[turn - 1], row_ssem.at[turn])
+        wait_all(sum_recv.at[turn - 1], row_ssem.at[turn - 1])
         wait_all(col_recv.at[turn], col_ssem.at[turn])
     wait_all(out_recv, out_sem.at[0])
     pltpu.make_async_copy(side_recv, side_recv, side_sem.at[0]).wait()
@@ -485,8 +499,8 @@
                 pltpu.VMEM((col_tiles, LANES), F32),
                 pltpu.VMEM((nx, col_tiles, LANES), F32),
                 pltpu.VMEM((col_tiles, LANES), F32),
-                pltpu.VMEM((row_tiles, LANES), F32),
-                pltpu.VMEM((ny, row_tiles, LANES), F32),
+                pltpu.VMEM((2, row_tiles // 2, LANES), F32),
+                pltpu.VMEM((2, ny, row_tiles // 2, LANES), F32),
                 pltpu.VMEM((SWEEPS - 1, row_tiles, LANES), BF16),
                 pltpu.VMEM((SWEEPS - 1, ny, row_tiles, LANES), BF16),
                 pltpu.VMEM((SWEEPS, col_tiles, LANES), F32),
@@ -498,8 +512,9 @@
                 pltpu.VMEM((LANES, width), BF16),
                 pltpu.VMEM((LANES, width), BF16),
                 dma((5,)),
-                dma((SWEEPS,)),
-                dma((SWEEPS,)),
+                dma((4,)),
+                dma((SWEEPS - 1,)),
+                dma((SWEEPS - 1,)),
                 dma((SWEEPS,)),
                 dma((SWEEPS,)),
                 dma((2,)),

time: 54.2 us -> 55.1 us (1.017)
  Pallas kernels: 53.2 us -> 54 us
    pallas_call x1, Pallas kernels: 53.2 us -> 54 us  [body(): pl.pallas_call(functools.partial(kernel, (nx, ny)), out_shape=jax.ShapeDt...]
where the time goes in v7:
time: 55.1 us; the launch traced here: 55 us
  Pallas kernels  54 us (98%)
  matrix products  0.95 us (2%)
    pallas_call x1, Pallas kernels, body(): pl.pallas_call(functools.partial(kernel, (nx, ny)), out_shape=jax.ShapeDt...  54 us

profile of v7, /device:TPU:1, one launch (start us, length us, event | category | flops | bytes accessed | tf_op | source)
XLA Modules:
  0.0 55.0 jit_solution(216145939331429836)
XLA Ops:
  0.0 0.0 copy-start
  0.0 54.0 %shard_map.46 = bf16[128,256]{1,0:T(8,128)(2,1)S(1)} custom-call(bf16[2048,128]{1,0:T(8,128)(2,1)} %bitcast.4, bf16[1024,128]{1,0:T(8,128)(2,1)} %bitcast.5, bf16[1024,128]{1,0:T(8,128)(2,1)} %bitcast.6), custom_call_target="tpu_custom_call" | custom-call | tf_op jit(solution)/shard_map/pallas_call | solution.py:475
  54.0 0.0 copy-done
  54.0 0.9 %convolution_convert_fusion = bf16[128,1024]{1,0:T(8,128)(2,1)} fusion(bf16[128,256]{1,0:T(8,128)(2,1)S(1)} %shard_map.46, bf16[256,2048]{1,0:T(8,128)(2,1)S(1)} %copy-done, s32[]{:T(128)S(6)} %select_n.3), kind=kOutput, calls=%fused_computation | convolution fusion | flops 67239936 | bytes 851972 | tf_op jit(solution)/shard_map/dot_general | solution.py:538
Async XLA Ops:
  0.0 54.0 %copy-start = (bf16[256,2048]{1,0:T(8,128)(2,1)S(1)}, bf16[256,2048]{1,0:T(8,128)(2,1)}, u32[]{:S(2)}) copy-start(bf16[256,2048]{1,0:T(8,128)(2,1)} %param.7) | copy-start | bytes 3145732

commit v8 on v6

--- a/solution.py
+++ b/solution.py
@@ -17,6 +17,13 @@
 
 def far_first(count):
     return sorted(range(count), key=lambda d: -min(d, count - d))
+
+
+def in_pairs(combine, parts):
+    while len(parts) > 1:
+        joined = [combine(*parts[n : n + 2]) for n in range(0, len(parts) - 1, 2)]
+        parts = joined + parts[len(parts) // 2 * 2 :]
+    return parts[0]
 
 
 def split_lhs(x):
@@ -119,6 +126,13 @@
             barrier, inc=1, device_id={"gx": col_peer(dy, dx)}, device_id_type=MESH
         )
     pl.semaphore_signal(barrier, inc=1, device_id={"gz": 1 - gz}, device_id_type=MESH)
+    for dz in range(1, nz):
+        pl.semaphore_signal(
+            barrier,
+            inc=1,
+            device_id={"gy": row_peer(dz, 0), "gz": 1 - gz},
+            device_id_type=MESH,
+        )
     beside = z * 2 + 1 - xl
     for dy, dx in col_peers:
         pl.semaphore_signal(
@@ -166,25 +180,21 @@
     pair_log = to_pair(log_send, log_recv, 4)
     pair_part = to_pair(part_send, part_recv, 5)
 
-    def ranked(n):
-        return jnp.where(n < nz // 2, n, nz + nz // 2 - 1 - n)
-
-    targets = [ranked(jnp.where(n >= ranked(z), n + 1, n)) for n in range(nz - 1)] + [z]
+    turned = 3 if nz >= 8 else 1
+
+    def ranked(n, shift):
+        late = jnp.where(n < nz // 2, n, nz + nz // 2 - 1 - n)
+        return jnp.where(n < turned, lax.rem(n + shift, turned), late)
+
+    rank = ranked(z, turned - 1)
+    targets = [ranked(jnp.where(n >= rank, n + 1, n), 1) for n in range(nz - 1)] + [z]
 
     def log_total(own, received):
-        biggest = own
-        for other in received:
-            biggest = jnp.maximum(biggest, other)
-        total = jnp.exp2(own - biggest)
-        for other in received:
-            total = total + jnp.exp2(other - biggest)
-        return biggest + jnp.log2(total)
+        biggest = in_pairs(jnp.maximum, [own, *received])
+        return biggest + jnp.log2(in_pairs(jnp.add, [jnp.exp2(x - biggest) for x in [own, *received]]))
 
     def plain_total(own, received):
-        total = own
-        for other in received:
-            total = total + other
-        return total
+        return in_pairs(jnp.add, [own, *received])
 
     loads[1].wait()
     loads[3].wait()
@@ -205,24 +215,23 @@
             preferred_element_type=F32,
         )
         s_ref[:, lanes] = scores
-        biggest, summed = None, None
+        tops, sums = [], []
         for jb in range(col_tiles):
             part = scores[jb * LANES : (jb + 1) * LANES].reshape(LANES // 8, 8, block)
             top = jnp.max(part, axis=0)
-            total = jnp.sum(jnp.exp2(part - top[None]), axis=0)
-            if biggest is None:
-                biggest, summed = top, total
-            else:
-                larger = jnp.maximum(biggest, top)
-                summed = summed * jnp.exp2(biggest - larger) + total * jnp.exp2(top - larger)
-                biggest = larger
+            tops.append(top)
+            sums.append(jnp.sum(jnp.exp2(part - top[None]), axis=0))
+        biggest = in_pairs(jnp.maximum, tops)
+        summed = in_pairs(
+            jnp.add, [total * jnp.exp2(top - biggest) for top, total in zip(tops, sums)]
+        )
         top = jnp.max(biggest, axis=0, keepdims=True)
         summed = jnp.sum(summed * jnp.exp2(biggest - top), axis=0, keepdims=True)
         local = top + jnp.log2(summed)
         for t in range(block // LANES):
             row_send[pl.ds(b * (block // LANES) + t, 1), :] = local[:, t * LANES : (t + 1) * LANES]
 
-    pl.semaphore_wait(barrier, len(row_peers) + 2 * len(col_peers) + 1)
+    pl.semaphore_wait(barrier, len(row_peers) + 2 * len(col_peers) + nz)
     send_all(row_send, row_recv, row_ssem.at[0], row_rsem.at[0], row_to)
     loads[4].wait()
     pair_keys[0].start()
@@ -412,40 +421,66 @@
             if n != nz - 1:
                 pltpu.make_async_remote_copy(
                     src_ref=out_send.at[n],
-                    dst_ref=out_recv.at[lax.rem(z - targets[n] + nz, nz)],
-                    send_sem=out_sem.at[0],
-                    recv_sem=out_sem.at[1],
-                    device_id={"gy": targets[n] * 2 + xl},
+                    dst_ref=out_recv.at[gz, lax.rem(z - targets[n] + nz, nz)],
+                    send_sem=out_sem.at[2],
+                    recv_sem=out_sem.at[gz],
+                    device_id={"gy": targets[n] * 2 + xl, "gz": 1},
                     device_id_type=MESH,
                 ).start()
-    wait_all(out_recv, out_sem.at[1])
-    total = out_send[nz - 1].astype(F32)
-    for slot in range(1, nz):
-        total = total + out_recv[slot].astype(F32)
-    weight = jnp.sum(total[width:], axis=0, keepdims=True)
-    head = (total[0:width] / weight).T.astype(BF16)
-    head_send[...] = head
-    swap = pltpu.make_async_remote_copy(
-        src_ref=head_send,
-        dst_ref=head_recv,
-        send_sem=head_sem.at[0],
-        recv_sem=head_sem.at[1],
-        device_id={"gz": 1 - gz},
-        device_id_type=MESH,
-    )
-    swap.start()
-    out_ref[:, pl.ds(pl.multiple_of(gz * width, width), width)] = head
+    def all_waited(view, sem):
+        pltpu.make_async_copy(view, view, sem).wait()
+
+    def head_of(pieces):
+        total = in_pairs(jnp.add, [piece.astype(F32) for piece in pieces])
+        weight = jnp.sum(total[width:], axis=0, keepdims=True)
+        return (total[0:width] / weight).T.astype(BF16)
+
+    others = out_recv.at[1, pl.ds(1, nz - 1)]
+
+    @pl.when(gz == 0)
+    def _():
+        own = pltpu.make_async_remote_copy(
+            src_ref=out_send.at[nz - 1],
+            dst_ref=out_recv.at[0, 0],
+            send_sem=head_sem.at[0],
+            recv_sem=out_sem.at[0],
+            device_id={"gz": 1},
+            device_id_type=MESH,
+        )
+        own.start()
+        own.wait_send()
+        all_waited(head_recv, head_sem.at[1])
+        out_ref[...] = head_recv[...]
+
+    @pl.when(gz == 1)
+    def _():
+        all_waited(others, out_sem.at[1])
+        head_send[:, width:] = head_of(
+            [out_send[nz - 1], *(out_recv[1, slot] for slot in range(1, nz))]
+        )
+        all_waited(out_recv.at[0], out_sem.at[0])
+        head_send[:, 0:width] = head_of([out_recv[0, slot] for slot in range(nz)])
+        swap = pltpu.make_async_remote_copy(
+            src_ref=head_send,
+            dst_ref=head_recv,
+            send_sem=head_sem.at[0],
+            recv_sem=head_sem.at[1],
+            device_id={"gz": 0},
+            device_id_type=MESH,
+        )
+        swap.start()
+        out_ref[...] = head_send[...]
+        swap.wait_send()
+
     wait_all(row_recv, row_ssem.at[0])
     wait_all(col_recv.at[0], col_ssem.at[0])
     for turn in range(1, SWEEPS):
         wait_all(sum_recv.at[turn - 1], row_ssem.at[turn])
         wait_all(col_recv.at[turn], col_ssem.at[turn])
-    wait_all(out_recv, out_sem.at[0])
+    all_waited(others, out_sem.at[2])
     pltpu.make_async_copy(side_recv, side_recv, side_sem.at[0]).wait()
     for copy in [*pair_keys, *pair_values, pair_log, pair_part]:
         copy.wait_send()
-    swap.wait()
-    out_ref[:, pl.ds(pl.multiple_of((1 - gz) * width, width), width)] = head_recv[...]
 
 
 def solution(mesh):
@@ -494,15 +529,15 @@
                 pltpu.VMEM((row_tiles, LANES), F32),
                 pltpu.VMEM((col_tiles, LANES), F32),
                 pltpu.VMEM((ny // 2, width + 16, LANES), BF16),
-                pltpu.VMEM((ny // 2, width + 16, LANES), BF16),
-                pltpu.VMEM((LANES, width), BF16),
-                pltpu.VMEM((LANES, width), BF16),
+                pltpu.VMEM((2, ny // 2, width + 16, LANES), BF16),
+                pltpu.VMEM((LANES, 2 * width), BF16),
+                pltpu.VMEM((LANES, 2 * width), BF16),
                 dma((5,)),
                 dma((SWEEPS,)),
                 dma((SWEEPS,)),
                 dma((SWEEPS,)),
                 dma((SWEEPS,)),
-                dma((2,)),
+                dma((3,)),
                 dma((2,)),
                 dma((6,)),
                 dma((6,)),

time: 54.2 us -> 55.5 us (1.024)
  Pallas kernels: 53.2 us -> 54.5 us
    pallas_call x1, Pallas kernels: 53.2 us -> 54.5 us  [body(): pl.pallas_call(functools.partial(kernel, (nx, ny)), out_shape=jax.ShapeDt...]
where the time goes in v8:
time: 55.5 us; the launch traced here: 55.4 us
  Pallas kernels  54.5 us (98%)
  matrix products  0.95 us (2%)
    pallas_call x1, Pallas kernels, body(): pl.pallas_call(functools.partial(kernel, (nx, ny)), out_shape=jax.ShapeDt...  54.5 us

profile of v8, /device:TPU:1, one launch (start us, length us, event | category | flops | bytes accessed | tf_op | source)
XLA Modules:
  0.0 55.4 jit_solution(11637488064415206360)
XLA Ops:
  0.0 0.0 copy-start
  0.0 54.5 %shard_map.46 = bf16[128,256]{1,0:T(8,128)(2,1)S(1)} custom-call(bf16[2048,128]{1,0:T(8,128)(2,1)} %bitcast.4, bf16[1024,128]{1,0:T(8,128)(2,1)} %bitcast.5, bf16[1024,128]{1,0:T(8,128)(2,1)} %bitcast.6), custom_call_target="tpu_custom_call" | custom-call | tf_op jit(solution)/shard_map/pallas_call | solution.py:496
  54.5 0.0 copy-done
  54.5 0.9 %convolution_convert_fusion = bf16[128,1024]{1,0:T(8,128)(2,1)} fusion(bf16[128,256]{1,0:T(8,128)(2,1)S(1)} %shard_map.46, bf16[256,2048]{1,0:T(8,128)(2,1)S(1)} %copy-done, s32[]{:T(128)S(6)} %select_n.3), kind=kOutput, calls=%fused_computation | convolution fusion | flops 67239936 | bytes 851972 | tf_op jit(solution)/shard_map/dot_general | solution.py:558
Async XLA Ops:
  0.0 54.5 %copy-start = (bf16[256,2048]{1,0:T(8,128)(2,1)S(1)}, bf16[256,2048]{1,0:T(8,128)(2,1)}, u32[]{:S(2)}) copy-start(bf16[256,2048]{1,0:T(8,128)(2,1)} %param.7) | copy-start | bytes 3145732

commit v9 on v6

--- a/solution.py
+++ b/solution.py
@@ -17,6 +17,13 @@
 
 def far_first(count):
     return sorted(range(count), key=lambda d: -min(d, count - d))
+
+
+def in_pairs(combine, parts):
+    while len(parts) > 1:
+        joined = [combine(*parts[n : n + 2]) for n in range(0, len(parts) - 1, 2)]
+        parts = joined + parts[len(parts) // 2 * 2 :]
+    return parts[0]
 
 
 def split_lhs(x):
@@ -172,19 +179,11 @@
     targets = [ranked(jnp.where(n >= ranked(z), n + 1, n)) for n in range(nz - 1)] + [z]
 
     def log_total(own, received):
-        biggest = own
-        for other in received:
-            biggest = jnp.maximum(biggest, other)
-        total = jnp.exp2(own - biggest)
-        for other in received:
-            total = total + jnp.exp2(other - biggest)
-        return biggest + jnp.log2(total)
+        biggest = in_pairs(jnp.maximum, [own, *received])
+        return biggest + jnp.log2(in_pairs(jnp.add, [jnp.exp2(x - biggest) for x in [own, *received]]))
 
     def plain_total(own, received):
-        total = own
-        for other in received:
-            total = total + other
-        return total
+        return in_pairs(jnp.add, [own, *received])
 
     loads[1].wait()
     loads[3].wait()
@@ -205,17 +204,16 @@
             preferred_element_type=F32,
         )
         s_ref[:, lanes] = scores
-        biggest, summed = None, None
+        tops, sums = [], []
         for jb in range(col_tiles):
             part = scores[jb * LANES : (jb + 1) * LANES].reshape(LANES // 8, 8, block)
             top = jnp.max(part, axis=0)
-            total = jnp.sum(jnp.exp2(part - top[None]), axis=0)
-            if biggest is None:
-                biggest, summed = top, total
-            else:
-                larger = jnp.maximum(biggest, top)
-                summed = summed * jnp.exp2(biggest - larger) + total * jnp.exp2(top - larger)
-                biggest = larger
+            tops.append(top)
+            sums.append(jnp.sum(jnp.exp2(part - top[None]), axis=0))
+        biggest = in_pairs(jnp.maximum, tops)
+        summed = in_pairs(
+            jnp.add, [total * jnp.exp2(top - biggest) for top, total in zip(tops, sums)]
+        )
         top = jnp.max(biggest, axis=0, keepdims=True)
         summed = jnp.sum(summed * jnp.exp2(biggest - top), axis=0, keepdims=True)
         local = top + jnp.log2(summed)

time: 54.2 us -> 54.2 us (level)
  no operation moved by 1% of the time
where the time goes in v9:
time: 54.2 us; the launch traced here: 54.1 us
  Pallas kernels  53.1 us (98%)
  matrix products  0.95 us (2%)
    pallas_call x1, Pallas kernels, body(): pl.pallas_call(functools.partial(kernel, (nx, ny)), out_shape=jax.ShapeDt...  53.1 us

profile of v9, /device:TPU:1, one launch (start us, length us, event | category | flops | bytes accessed | tf_op | source)
XLA Modules:
  0.0 54.1 jit_solution(1612127712564021357)
XLA Ops:
  0.0 0.0 copy-start
  0.0 53.1 %shard_map.46 = bf16[128,256]{1,0:T(8,128)(2,1)S(1)} custom-call(bf16[2048,128]{1,0:T(8,128)(2,1)} %bitcast.4, bf16[1024,128]{1,0:T(8,128)(2,1)} %bitcast.5, bf16[1024,128]{1,0:T(8,128)(2,1)} %bitcast.6), custom_call_target="tpu_custom_call" | custom-call | tf_op jit(solution)/shard_map/pallas_call | solution.py:459
  53.1 0.0 copy-done
  53.1 0.9 %convolution_convert_fusion = bf16[128,1024]{1,0:T(8,128)(2,1)} fusion(bf16[128,256]{1,0:T(8,128)(2,1)S(1)} %shard_map.46, bf16[256,2048]{1,0:T(8,128)(2,1)S(1)} %copy-done, s32[]{:T(128)S(6)} %select_n.3), kind=kOutput, calls=%fused_computation | convolution fusion | flops 67239936 | bytes 851972 | tf_op jit(solution)/shard_map/dot_general | solution.py:521
Async XLA Ops:
  0.0 53.1 %copy-start = (bf16[256,2048]{1,0:T(8,128)(2,1)S(1)}, bf16[256,2048]{1,0:T(8,128)(2,1)}, u32[]{:S(2)}) copy-start(bf16[256,2048]{1,0:T(8,128)(2,1)} %param.7) | copy-start | bytes 3145732

commit v10 on v6

--- a/solution.py
+++ b/solution.py
@@ -384,8 +384,9 @@
             line = col_vec[t : t + 1, :]
         else:
             line = side[t - col_tiles : t - col_tiles + 1, :]
-        val_lhs[0:width, lanes] = (val_lhs[0:width, lanes].astype(F32) * line).astype(BF16)
-        val_lhs[width : width + 16, lanes] = split_lhs(line)
+        rounded = line.astype(BF16)
+        val_lhs[0:width, lanes] = val_lhs[0:width, lanes] * rounded
+        val_lhs[width : width + 16, lanes] = split_lhs(rounded.astype(F32))
     tail = lax.broadcasted_iota(jnp.int32, (16, LANES), 0)
 
     def product(m):

time: 54.2 us -> 54.2 us (level)
  no operation moved by 1% of the time
where the time goes in v10:
time: 54.2 us; the launch traced here: 54.1 us
  Pallas kernels  53.2 us (98%)
  matrix products  0.95 us (2%)
    pallas_call x1, Pallas kernels, body(): pl.pallas_call(functools.partial(kernel, (nx, ny)), out_shape=jax.ShapeDt...  53.2 us

profile of v10, /device:TPU:1, one launch (start us, length us, event | category | flops | bytes accessed | tf_op | source)
XLA Modules:
  0.0 54.1 jit_solution(4095821784927541602)
XLA Ops:
  0.0 0.0 copy-start
  0.0 53.2 %shard_map.46 = bf16[128,256]{1,0:T(8,128)(2,1)S(1)} custom-call(bf16[2048,128]{1,0:T(8,128)(2,1)} %bitcast.4, bf16[1024,128]{1,0:T(8,128)(2,1)} %bitcast.5, bf16[1024,128]{1,0:T(8,128)(2,1)} %bitcast.6), custom_call_target="tpu_custom_call" | custom-call | tf_op jit(solution)/shard_map/pallas_call | solution.py:462
  53.2 0.0 copy-done
  53.2 0.9 %convolution_convert_fusion = bf16[128,1024]{1,0:T(8,128)(2,1)} fusion(bf16[128,256]{1,0:T(8,128)(2,1)S(1)} %shard_map.46, bf16[256,2048]{1,0:T(8,128)(2,1)S(1)} %copy-done, s32[]{:T(128)S(6)} %select_n.3), kind=kOutput, calls=%fused_computation | convolution fusion | flops 67239936 | bytes 851972 | tf_op jit(solution)/shard_map/dot_general | solution.py:524
Async XLA Ops:
  0.0 53.2 %copy-start = (bf16[256,2048]{1,0:T(8,128)(2,1)S(1)}, bf16[256,2048]{1,0:T(8,128)(2,1)}, u32[]{:S(2)}) copy-start(bf16[256,2048]{1,0:T(8,128)(2,1)} %param.7) | copy-start | bytes 3145732
